TPU v7x, 256 devices: a whole 4x4x8 slice. The times are simulated.
256 devices in a mesh: dop: 32 (over z, y), slow: 8 (over x, core).
Axes of the slice: x: 4, y: 4, z: 8, core: 2. Of those that a mesh axis runs over, the one named last changes fastest.
Arguments:
- profiles: bfloat16 [64, 2, 1024, 2048], P('slow', None, 'dop'), may hold values from -6 to 6
- range_walk: int32 [2048], replicated, may hold values from -32 to 32
- band_order: int32 [256], replicated, may hold values from 0 to 255, each once
Outputs:
- ambiguity: float32 [2048, 1024], P(('dop', 'slow'))
Inputs may be any that keep to these rules, and one draw needn't show every extreme that they name: `band_order`: each band number appears exactly once.
All inputs are finite; a program needn't handle non-finite values.
Results may differ from a plain program's by a relative error of at most 0.00067.
Values sent between devices are 32-bit elements; how exact they have to be, the bound alone decides.
No kernel may reach another device: no remote copies, remote signals or barrier semaphores. Data moves between devices by JAX's collectives and lax.ppermute only.
A program may use at most 64 MiB of HBM per device.

v0:
```python
import math

import jax
import jax.numpy as jnp
from jax import lax
from jax.sharding import PartitionSpec as P

WALK = 32


def from_behind(value, axis, steps):
    count = lax.axis_size(axis)
    leading, last = (max(0, -steps), min(count, count - steps))
    return lax.ppermute(value, axis, [(source, source + steps) for source in range(leading, last)])


def cut_along(x, dim, devices):
    before, after = (x.shape[:dim], x.shape[dim + 1 :])
    return jnp.moveaxis(x.reshape(*before, devices, -1, *after), dim, 0)


def summed_on_arrival(x, axis, dim):
    tiles = cut_along(x, dim, lax.axis_size(axis))
    arrived = lax.all_to_all(tiles, axis, split_axis=0, concat_axis=0, tiled=True)
    return arrived.sum(axis=0)


def fourier_tables(length):
    counter = jnp.arange(length, dtype=jnp.int32)
    phases = counter[:, None] * counter[None, :] % length
    angles = phases.astype(jnp.float32) * (2.0 * math.pi / length)
    return (jnp.cos(angles).astype(jnp.bfloat16), jnp.sin(angles).astype(jnp.bfloat16))


def batch_powers(block, cosine, sine_table):
    count = block.shape[0]
    delays = block.shape[2]
    bins = block.shape[3]
    stacked = block.reshape(count * 2 * delays, bins)
    first = jnp.dot(stacked, cosine, preferred_element_type=jnp.float32).reshape(
        count, 2, delays, bins
    )
    second = jnp.dot(stacked, sine_table, preferred_element_type=jnp.float32).reshape(
        count, 2, delays, bins
    )
    real_part = first[:, 0] + second[:, 1]
    imag_part = first[:, 1] - second[:, 0]
    return real_part * real_part + imag_part * imag_part


def walk_align(padded, offsets, out_rows, reach):
    moves = offsets + reach
    levels = max(1, (2 * reach).bit_length())
    needed = out_rows + (1 << levels) - 1
    current = jnp.pad(padded, ((0, 0), (0, needed - padded.shape[1]), (0, 0)))
    for level in range(levels):
        stride = 1 << level
        taken = (moves // stride % 2 == 1)[:, None, :]
        current = jnp.where(taken, current[:, stride:], current[:, :-stride])
    return current


def permute_bands(values, band_order, band_count):
    picker = (band_order[:, None] == jnp.arange(band_count, dtype=jnp.int32)[None, :]).astype(
        jnp.float32
    )
    return jnp.einsum("bc,...cj->...bj", picker, values, precision=lax.Precision.HIGHEST)


def on_device(profiles, range_walk, band_order):
    batch_count = profiles.shape[0]
    local_rows = profiles.shape[2]
    doppler_bins = profiles.shape[3]
    dop_count = lax.axis_size("dop")
    slow_count = lax.axis_size("slow")
    total_batches = batch_count * slow_count
    band_count = dop_count * slow_count
    band_rows = doppler_bins // band_count
    scale = 1.0 / (total_batches * doppler_bins)
    cosine, sine_table = fourier_tables(doppler_bins)
    powers = batch_powers(profiles, cosine, sine_table)
    batches = lax.axis_index("slow") * batch_count + jnp.arange(batch_count, dtype=jnp.int32)
    offsets = range_walk[None, :] * batches[:, None] // total_batches
    widened = jnp.pad(powers, ((0, 0), (2 * WALK, 2 * WALK), (0, 0)))
    gathered = jnp.sum(walk_align(widened, offsets, local_rows + 2 * WALK, WALK), axis=0)
    lower_rim = gathered[:WALK]
    upper_rim = gathered[local_rows + WALK :]
    own_rows = gathered[WALK : local_rows + WALK]
    from_below = from_behind(upper_rim, "dop", 1)
    from_above = from_behind(lower_rim, "dop", -1)
    own_rows = own_rows.at[:WALK].add(from_below)
    own_rows = own_rows.at[local_rows - WALK :].add(from_above)
    partial_value = own_rows * scale
    ordered = permute_bands(
        partial_value.reshape(local_rows, band_count, band_rows), band_order, band_count
    )
    grouped = ordered.reshape(local_rows, dop_count, slow_count, band_rows).transpose(0, 2, 1, 3)
    grouped = grouped.reshape(local_rows, doppler_bins)
    summed = summed_on_arrival(grouped, "slow", 1)
    result = lax.all_to_all(summed, "dop", split_axis=1, concat_axis=0, tiled=True)
    return result.T


def solution(mesh):
    placed = (P("slow", None, "dop", None), P(), P())
    return jax.shard_map(
        on_device, mesh=mesh, in_specs=placed, out_specs=P(("dop", "slow"), None), check_vma=False
    )
```

profile of v0, /device:TPU:1, one launch (start us, length us, event | category | flops | bytes accessed | tf_op | source)
XLA Modules:
  0.0 232.3 jit_solution(15600399316770278802)
XLA Ops:
  0.0 0.0 copy-start
  0.0 1.6 copy-done
  1.6 63.9 %fusion.7 = f32[2048,512]{0,1:T(8,128)} fusion(bf16[512,2048]{1,0:T(8,128)(2,1)S(1)} %bitcast.66), kind=kOutput, calls=%fused_computation.19 | convolution fusion | flops 4357881856 | bytes 6291456 | tf_op jit(solution)/shard_map/dot_general | solution.py:40
  65.5 0.0 copy-start.2
  65.5 64.4 %fusion.8 = f32[2048,512]{0,1:T(8,128)} fusion(bf16[512,2048]{1,0:T(8,128)(2,1)S(1)} %bitcast.65), kind=kOutput, calls=%fused_computation.20 | convolution fusion | flops 4357881856 | bytes 6291456 | tf_op jit(solution)/shard_map/dot_general | solution.py:43
  129.9 0.0 copy-done.2
  129.9 0.5 fusion.27
  130.4 4.5 %fusion.15 = f32[8,32,2048]{2,1,0:T(8,128)S(1)} fusion(f32[8,2,32,2048]{3,2,1,0:T(8,128)} %bitcast.71, f32[8,2,32,2048]{3,2,1,0:T(8,128)} %bitcast.70), kind=kLoop, calls=%fused_computation.27 | loop fusion | flops 2621440 | bytes 10485760 | tf_op jit(solution)/shard_map/add | solution.py:48
  134.9 7.2 %fusion.6 = f32[8,222,2048]{2,1,0:T(8,128)} fusion(f32[8,32,2048]{2,1,0:T(8,128)S(1)} %fusion.15, pred[8,2048]{1,0:T(8,128)(4,1)S(1)} %get-tuple-element.51), kind=kLoop, calls=%fused_computation.13 | loop fusion | flops 3637248 | bytes 16662528 | tf_op jit(solution)/shard_map/jit(_where)/select_n | solution.py:59
  142.1 10.7 %slice_select_fusion = f32[8,220,2048]{2,1,0:T(8,128)S(1)} fusion(f32[8,222,2048]{2,1,0:T(8,128)} %fusion.6, pred[8,2048]{1,0:T(8,128)(4,1)S(1)} %get-tuple-element.53), kind=kLoop, calls=%fused_computation.14 | loop fusion | flops 3604480 | bytes 43270144 | tf_op jit(solution)/shard_map/jit(_where)/select_n | solution.py:59
  152.8 3.4 %slice_select_fusion.1 = f32[8,216,2048]{2,1,0:T(8,128)S(1)} fusion(f32[8,220,2048]{2,1,0:T(8,128)S(1)} %slice_select_fusion, pred[8,2048]{1,0:T(8,128)(4,1)S(1)} %get-tuple-element.49), kind=kLoop, calls=%fused_computation.15 | loop fusion | flops 3538944 | bytes 42483712 | tf_op jit(solution)/shard_map/jit(_where)/select_n | solution.py:59
  156.2 6.7 %slice_select_fusion.2 = f32[8,208,2048]{2,1,0:T(8,128)} fusion(f32[8,216,2048]{2,1,0:T(8,128)S(1)} %slice_select_fusion.1, pred[8,2048]{1,0:T(8,128)(4,1)S(1)} %get-tuple-element.52), kind=kLoop, calls=%fused_computation.16 | loop fusion | flops 3407872 | bytes 40910848 | tf_op jit(solution)/shard_map/jit(_where)/select_n | solution.py:59
  162.9 9.4 %slice_select_fusion.3 = f32[8,192,2048]{2,1,0:T(8,128)S(1)} fusion(f32[8,208,2048]{2,1,0:T(8,128)} %slice_select_fusion.2, pred[8,2048]{1,0:T(8,128)(4,1)S(1)} %get-tuple-element.50), kind=kLoop, calls=%fused_computation.17 | loop fusion | flops 3145728 | bytes 37765120 | tf_op jit(solution)/shard_map/jit(_where)/select_n | solution.py:59
  172.3 3.7 %slice_select_fusion.4 = f32[8,160,2048]{2,1,0:T(8,128)S(1)} fusion(f32[8,192,2048]{2,1,0:T(8,128)S(1)} %slice_select_fusion.3, pred[8,2048]{1,0:T(8,128)(4,1)S(1)} %get-tuple-element.48), kind=kLoop, calls=%fused_computation.18 | loop fusion | flops 2621440 | bytes 31473664 | tf_op jit(solution)/shard_map/jit(_where)/select_n | solution.py:59
  176.0 0.0 copy-start.3
  176.0 0.0 copy-start.1
  176.0 1.2 fusion.11
  177.3 4.0 %collective-permute-start = (f32[32,2048]{1,0:T(8,128)S(1)}, f32[32,2048]{1,0:T(8,128)S(1)}, u32[]{:S(2)}, u32[]{:S(2)}) collective-permute-start(f32[32,2048]{1,0:T(8,128)S(1)} %get-tuple-element.45), channel_id=1, source_target_pairs={{0,8},{8,16},{16,24},{24,32},{32,40},{40,48},{48,56},{56,64},{64,7... | collective-permute-start | bytes 786440 | tf_op jit(solution)/shard_map/ppermute | solution.py:14
  181.4 1.3 collective-permute-start.1
  182.7 3.7 %collective-permute-done = f32[32,2048]{1,0:T(8,128)S(1)} collective-permute-done((f32[32,2048]{1,0:T(8,128)S(1)}, f32[32,2048]{1,0:T(8,128)S(1)}, u32[]{:S(2)}, u32[]{:S(2)}) %collective-permute-start) | collective-permute-done | bytes 262176 | tf_op jit(solution)/shard_map/ppermute | solution.py:14
  186.3 3.8 %collective-permute-done.1 = f32[32,2048]{1,0:T(8,128)S(1)} collective-permute-done((f32[32,2048]{1,0:T(8,128)S(1)}, f32[32,2048]{1,0:T(8,128)S(1)}, u32[]{:S(2)}, u32[]{:S(2)}) %collective-permute-start.1) | collective-permute-done | bytes 262176 | tf_op jit(solution)/shard_map/ppermute | solution.py:14
  190.2 0.3 copy.25
  190.5 0.4 copy.26
  191.0 0.0 copy-done.3
  191.0 1.1 convolution_bitcast_fusion
  192.1 1.4 copy.27
  193.4 1.1 copy.37
  194.5 1.5 copy.29
  196.0 12.4 %all_to_all.24 = f32[8,32,256]{2,1,0:T(8,128)S(1)} all-to-all(f32[8,32,256]{2,1,0:T(8,128)S(1)} %copy.29), channel_id=1, replica_groups=mesh['dop'=32,'slow'=8] {'slow'}, dimensions={0} | all-to-all | bytes 524288 | tf_op jit(solution)/shard_map/all_to_all | solution.py:24
  208.4 0.1 copy.30
  208.5 0.1 reshape.392
  208.7 21.5 %all_to_all.25 = f32[32,1,256]{2,1,0:T(1,128)S(1)} all-to-all(f32[32,1,256]{2,1,0:T(1,128)S(1)} %reshape.392), channel_id=1, replica_groups=mesh['dop'=32,'slow'=8] {'dop'}, dimensions={0} | all-to-all | bytes 65536 | tf_op jit(solution)/shard_map/all_to_all | solution.py:100
  230.2 0.5 broadcast.746
  230.7 0.7 reduce.6
  231.4 0.1 reshape.393
  231.6 0.7 all_to_all.21
  232.3 0.0 copy-done.1
  (7 shorter events, 0.1 us)
Async XLA Ops:
  0.0 1.6 copy-start
  65.5 64.4 %copy-start.2 = (s32[2048]{0:T(1024)S(1)}, s32[2048]{0:T(1024)}, u32[]{:S(2)}) copy-start(s32[2048]{0:T(1024)} %param.12) | copy-start | bytes 24580
  176.0 14.9 %copy-start.3 = (s32[256]{0:T(256)S(1)}, s32[256]{0:T(256)}, u32[]{:S(2)}) copy-start(s32[256]{0:T(256)} %param.13) | copy-start | bytes 3076
  176.0 56.3 %copy-start.1 = (bf16[8,2,32,2048]{3,2,1,0:T(8,128)(2,1)S(1)}, bf16[8,2,32,2048]{3,2,1,0:T(8,128)(2,1)}, u32[]{:S(2)}) copy-start(bf16[8,2,32,2048]{3,2,1,0:T(8,128)(2,1)} %param.11) | copy-start | bytes 6291460
  177.3 9.0 %collective-permute-start = (f32[32,2048]{1,0:T(8,128)S(1)}, f32[32,2048]{1,0:T(8,128)S(1)}, u32[]{:S(2)}, u32[]{:S(2)}) collective-permute-start(f32[32,2048]{1,0:T(8,128)S(1)} %get-tuple-element.45), channel_id=1, source_target_pairs={{0,8},{8,16},{16,24},{24,32},{32,40},{40,48},{48,56},{56,64},{64,7... | collective-permute-start | bytes 786440 | tf_op jit(solution)/shard_map/ppermute | solution.py:14
  181.4 8.8 %collective-permute-start.1 = (f32[32,2048]{1,0:T(8,128)S(1)}, f32[32,2048]{1,0:T(8,128)S(1)}, u32[]{:S(2)}, u32[]{:S(2)}) collective-permute-start(f32[32,2048]{1,0:T(8,128)S(1)} %get-tuple-element.46), channel_id=1, source_target_pairs={{8,0},{16,8},{24,16},{32,24},{40,32},{48,40},{56,48},{64,56},{72,6... | collective-permute-start | bytes 786440 | tf_op jit(solution)/shard_map/ppermute | solution.py:14
where the time goes:
time: 233 us; the launch traced here: 232 us
  matrix products  129 us (55%)
  other arithmetic  48.1 us (21%)
  blocking collectives  33.9 us (15%)
  local copies, waits for them, and re-layouts  7.89 us (3%)
  waiting for transfers between devices  7.5 us (3%)
  starting transfers between devices  5.33 us (2%)
    dot_general x1, matrix products, batch_powers(): jnp.dot(stacked, sine_table, preferred_element_type=jnp.float32)  64.4 us
    dot_general x1, matrix products, batch_powers(): jnp.dot(stacked, cosine, preferred_element_type=jnp.float32)  63.9 us
    select_n x6, other arithmetic, walk_align(): current = jnp.where(taken, current[:, stride:], current[:, :-stride])  41 us
    all_to_all x1, blocking collectives, on_device(): lax.all_to_all(summed, 'dop', split_axis=1, concat_axis=0, tiled=True)  21.5 us
    all_to_all x1, blocking collectives, summed_on_arrival(): lax.all_to_all(tiles, axis, split_axis=0, concat_axis=0, tiled=True)  12.4 us
    ppermute x2, waiting for transfers between devices, from_behind(): lax.ppermute(value, axis, [(source, source + steps) for source in range(l...  7.5 us
    ppermute x2, starting transfers between devices, from_behind(): lax.ppermute(value, axis, [(source, source + steps) for source in range(l...  5.33 us
  transfers between devices with their start and end apart: 2, of which 2 were waited for; matrix products, arithmetic and copies ran while one was open for 0% of the time, Pallas kernels for 0%

commit v1 on v0

v1 whole, which is shorter than its diff:
```python
import functools
import math

import jax
import jax.numpy as jnp
from jax import lax
from jax.experimental import pallas as pl
from jax.experimental.pallas import tpu as pltpu
from jax.sharding import PartitionSpec as P

WALK = 32
F = 2048
BANDS = 256
ROWS = 32
PER = 8
WIN = 40
SCALE = 1.0 / (64 * F)


def shifted(value, rows):
    if rows == 0:
        return value
    return pltpu.roll(value, rows, 0)


def spectra_kernel(slow_ref, x_ref, order_ref, walk_ref, out_ref, hi_ref, lo_ref, w_ref, kept_ref):
    slow = slow_ref[0]
    pulse = lax.broadcasted_iota(jnp.int32, (BANDS, BANDS), 0)
    turns = (pulse * order_ref[...]) & (BANDS - 1)
    angle = turns.astype(jnp.float32) * (2.0 * math.pi / BANDS)
    band_cos = jnp.cos(angle)
    band_sin = jnp.sin(angle)
    rows512 = lax.broadcasted_iota(jnp.int32, (512, 1), 0)
    walks = walk_ref[...]
    first = (walks * (8 * slow)) >> 6
    lead = jnp.where(walks >= 0, 4, 0)
    moves = [lead - (((walks * (8 * slow + g)) >> 6) - first) for g in range(PER)]
    for q in range(4):
        for g in range(PER):
            part = [
                [x_ref[g, c, :, k * 512 : (k + 1) * 512].astype(jnp.float32) for k in range(4)]
                for c in range(2)
            ]
            re, im = part
            if q % 2 == 0:
                zr = (re[0] + re[2]) + (re[1] + re[3]) * (1.0 if q == 0 else -1.0)
                zi = (im[0] + im[2]) + (im[1] + im[3]) * (1.0 if q == 0 else -1.0)
            else:
                sign = 1.0 if q == 1 else -1.0
                zr = (re[0] - re[2]) + (im[1] - im[3]) * sign
                zi = (im[0] - im[2]) - (re[1] - re[3]) * sign
            rh = zr.astype(jnp.bfloat16)
            ih = zi.astype(jnp.bfloat16)
            rl = (zr - rh.astype(jnp.float32)).astype(jnp.bfloat16)
            il = (zi - ih.astype(jnp.float32)).astype(jnp.bfloat16)
            up = slice(g * ROWS, (g + 1) * ROWS)
            down = slice(256 + g * ROWS, 256 + (g + 1) * ROWS)
            hi_ref[q, up, 0:512] = rh
            hi_ref[q, up, 512:1024] = ih
            hi_ref[q, down, 0:512] = ih
            hi_ref[q, down, 512:1024] = -rh
            lo_ref[q, up, 0:512] = rl
            lo_ref[q, up, 512:1024] = il
            lo_ref[q, down, 0:512] = il
            lo_ref[q, down, 512:1024] = -rl
        for jj in range(2):
            j = q + 4 * jj
            fine = ((rows512 * j) & (F - 1)).astype(jnp.float32) * (2.0 * math.pi / F)
            fine_cos = jnp.cos(fine)
            fine_sin = jnp.sin(fine)
            for half in range(2):
                fc = fine_cos[half * 256 : (half + 1) * 256]
                fs = fine_sin[half * 256 : (half + 1) * 256]
                at = half * 256
                w_ref[j, at : at + 256, :] = (band_cos * fc - band_sin * fs).astype(jnp.bfloat16)
                w_ref[j, 512 + at : 512 + at + 256, :] = (band_sin * fc + band_cos * fs).astype(
                    jnp.bfloat16
                )
            w = w_ref[j]
            spec = jnp.dot(hi_ref[q], w, preferred_element_type=jnp.float32)
            spec = spec + jnp.dot(lo_ref[q], w, preferred_element_type=jnp.float32)
            powers = spec[:256] * spec[:256] + spec[256:] * spec[256:]
            classes = [jnp.zeros((ROWS, BANDS), jnp.float32) for _ in range(5)]
            for g in range(PER):
                own = powers[g * ROWS : (g + 1) * ROWS]
                move = moves[g][j : j + 1, :]
                for k in range(5):
                    classes[k] = classes[k] + jnp.where(move == k, own, 0.0)
            rim = jnp.zeros((WIN - ROWS, BANDS), jnp.float32)
            total = None
            for k in range(5):
                piece = shifted(jnp.concatenate([classes[k], rim], axis=0), k)
                total = piece if total is None else total + piece
            kept_ref[j] = total
    lane = lax.broadcasted_iota(jnp.int32, (WIN, 128), 1) // 32
    for quad in range(2):
        for tile in range(2):
            held = [kept_ref[4 * tile + c, :, quad * 128 : (quad + 1) * 128] for c in range(4)]
            for s in range(4):
                result = None
                for c in range(4):
                    turned = held[c]
                    if c != s:
                        turned = pltpu.roll(turned, ((c - s) % 4) * 32, 1)
                    result = turned if result is None else jnp.where(lane == c, turned, result)
                out_ref[4 * quad + s, :, tile * 128 : (tile + 1) * 128] = result


def slow_kernel(x_ref, walk_ref, out_ref, turned_ref):
    walks = walk_ref[...]
    base = jnp.where(walks >= 0, 28, 32)
    for tile in range(2):
        lanes = slice(tile * 128, (tile + 1) * 128)
        total = jnp.zeros((96, 128), jnp.float32)
        for source in range(8):
            move = base - ((walks * source) >> 3)
            current = x_ref[source, :, lanes]
            rows = 48
            current = jnp.concatenate([current, jnp.zeros((rows - WIN, 128), jnp.float32)], axis=0)
            for bit in range(6):
                taken = ((move >> bit) & 1)[:, lanes] == 1
                if bit >= 3:
                    pad = jnp.zeros((1 << bit, 128), jnp.float32)
                    low = jnp.concatenate([current, pad], axis=0)
                    high = jnp.concatenate([pad, current], axis=0)
                    if low.shape[0] > 96:
                        low, high = low[:96], high[:96]
                    current = jnp.where(taken, high, low)
                else:
                    current = jnp.where(taken, pltpu.roll(current, 1 << bit, 0), current)
            total = total + current[:96]
        total = jnp.concatenate([total, jnp.zeros((32, 128), jnp.float32)], axis=0) * SCALE
        turned_ref[lanes, :] = total.T
    for block in range(32):
        out_ref[block] = turned_ref[pl.ds(block, 8, stride=32), :]


def join_kernel(x_ref, out_ref):
    lane = lax.broadcasted_iota(jnp.int32, (8, 128), 1)
    for v in range(8):
        total = None
        for step in range(-1, 5):
            block = 4 * v + step
            if block < 0 or block >= 32:
                continue
            offset = 32 * (step - 1)
            piece = x_ref[block]
            if offset != 0:
                piece = pltpu.roll(piece, offset % 128, 1)
            if offset < 0:
                piece = jnp.where(lane < 96 + offset, piece, 0.0)
            elif offset > 0:
                piece = jnp.where(lane >= offset, piece, 0.0)
            total = piece if total is None else total + piece
        out_ref[:, v * 128 : (v + 1) * 128] = total


VM = pl.BlockSpec(memory_space=pltpu.VMEM)
SM = pl.BlockSpec(memory_space=pltpu.SMEM)


def on_device(profiles, range_walk, band_order):
    slow = lax.axis_index("slow")
    order = band_order.reshape(32, 8).T.reshape(1, BANDS)
    walks = jnp.take(range_walk.reshape(BANDS, 8), order[0], axis=0).T
    sums = pl.pallas_call(
        spectra_kernel,
        out_shape=jax.ShapeDtypeStruct((8, WIN, BANDS), jnp.float32),
        in_specs=[SM, VM, VM, VM],
        out_specs=VM,
        scratch_shapes=[
            pltpu.VMEM((4, 512, 1024), jnp.bfloat16),
            pltpu.VMEM((4, 512, 1024), jnp.bfloat16),
            pltpu.VMEM((8, 1024, 256), jnp.bfloat16),
            pltpu.VMEM((8, WIN, BANDS), jnp.float32),
        ],
    )(slow.reshape(1), profiles, order, walks)
    gathered = lax.all_to_all(sums, "slow", split_axis=0, concat_axis=0, tiled=True)
    own = lax.dynamic_slice(walks, (0, slow * 32), (8, 32)).reshape(1, BANDS)
    blocks = pl.pallas_call(
        slow_kernel,
        out_shape=jax.ShapeDtypeStruct((32, 8, 128), jnp.float32),
        in_specs=[VM, VM],
        out_specs=VM,
        scratch_shapes=[pltpu.VMEM((BANDS, 128), jnp.float32)],
    )(gathered, own)
    arrived = lax.all_to_all(blocks, "dop", split_axis=0, concat_axis=0, tiled=True)
    return pl.pallas_call(
        join_kernel,
        out_shape=jax.ShapeDtypeStruct((8, 1024), jnp.float32),
        in_specs=[VM],
        out_specs=VM,
    )(arrived)


def solution(mesh):
    placed = (P("slow", None, "dop", None), P(), P())
    return jax.shard_map(
        on_device, mesh=mesh, in_specs=placed, out_specs=P(("dop", "slow"), None), check_vma=False
    )
```

time: 233 us -> 59.4 us (0.25)
  matrix products: 129 us -> 0 us
  other arithmetic: 48.1 us -> 0.64 us
  Pallas kernels: 0 us -> 20.7 us
  blocking collectives: 33.9 us -> 20 us
  local copies, waits for them, and re-layouts: 7.89 us -> 4.63 us
    dot_general x3 -> x0, matrix products: 129 us -> none  [the longest x1 64.4 us: batch_powers(): jnp.dot(stacked, sine_table, preferred_element_type=jnp.float32)]
    select_n x6 -> x3, other arithmetic: 41 us -> 0.63 us  [on_device(): walks = jnp.take(range_walk.reshape(BANDS, 8), order[0], axis=0).T]
    pallas_call x0 -> x3, Pallas kernels: none -> 20.7 us  [the longest x1 16.9 us: on_device(): pl.pallas_call(spectra_kernel, out_shape=jax.ShapeDtypeStruct((8, WIN, BA...]
    all_to_all x2 -> x1, blocking collectives: 33.9 us -> 20 us  [on_device(): lax.all_to_all(blocks, 'dop', split_axis=0, concat_axis=0, tiled=True)]
    ppermute x2 -> x0, waiting for transfers between devices: 7.5 us -> none  [from_behind(): lax.ppermute(value, axis, [(source, source + steps) for source in range(l...]
    all_to_all x0 -> x1, starting transfers between devices: none -> 6.53 us  [on_device(): lax.all_to_all(sums, 'slow', split_axis=0, concat_axis=0, tiled=True)]
    all_to_all x0 -> x1, waiting for transfers between devices: none -> 6.39 us  [on_device(): lax.all_to_all(sums, 'slow', split_axis=0, concat_axis=0, tiled=True)]
    ppermute x2 -> x0, starting transfers between devices: 5.33 us -> none  [from_behind(): lax.ppermute(value, axis, [(source, source + steps) for source in range(l...]
  transfers between devices with their start and end apart: 2 -> 1, of which waited for: 2 -> 1; matrix products, arithmetic and copies ran while one was open for 0% -> 1% of each run, Pallas kernels for 0% -> 0%
where the time goes in v1:
time: 59.4 us; the launch traced here: 58.9 us
  Pallas kernels  20.7 us (35%)
  blocking collectives  20 us (34%)
  starting transfers between devices  6.53 us (11%)
  waiting for transfers between devices  6.39 us (11%)
  local copies, waits for them, and re-layouts  4.63 us (8%)
  other arithmetic  0.64 us (1%)
    all_to_all x1, blocking collectives, on_device(): lax.all_to_all(blocks, 'dop', split_axis=0, concat_axis=0, tiled=True)  20 us
    pallas_call x1, Pallas kernels, on_device(): pl.pallas_call(spectra_kernel, out_shape=jax.ShapeDtypeStruct((8, WIN, BA...  16.9 us
    all_to_all x1, starting transfers between devices, on_device(): lax.all_to_all(sums, 'slow', split_axis=0, concat_axis=0, tiled=True)  6.53 us
    all_to_all x1, waiting for transfers between devices, on_device(): lax.all_to_all(sums, 'slow', split_axis=0, concat_axis=0, tiled=True)  6.39 us
    pallas_call x1, Pallas kernels, on_device(): pl.pallas_call(slow_kernel, out_shape=jax.ShapeDtypeStruct((32, 8, 128),...  2.18 us
    pallas_call x1, Pallas kernels, on_device(): pl.pallas_call(join_kernel, out_shape=jax.ShapeDtypeStruct((8, 1024), jnp...  1.63 us
    reshape x2, local copies, waits for them, and re-layouts, on_device(): order = band_order.reshape(32, 8).T.reshape(1, BANDS)  1.39 us
  transfers between devices with their start and end apart: 1, of which 1 were waited for; matrix products, arithmetic and copies ran while one was open for 1% of the time, Pallas kernels for 0%

profile of v1, /device:TPU:1, one launch (start us, length us, event | category | flops | bytes accessed | tf_op | source)
XLA Modules:
  0.0 58.9 jit_solution(13522832166170914254)
XLA Ops:
  0.0 0.8 %reshape.50 = s32[32,8]{1,0:T(8,128)S(1)} reshape(s32[256]{0:T(256)} %param.5) | data formatting | bytes 2048 | tf_op jit(solution)/shard_map/reshape | solution.py:164
  0.8 0.1 copy.7
  0.8 0.1 squeeze_reshape.6
  0.9 0.1 squeeze_reshape.5
  1.0 0.6 %reshape.51.order_ref = s32[1,256]{1,0:T(1,128)} reshape(s32[8,32]{1,0:T(8,128)S(1)} %copy.7) | data formatting | bytes 2048 | tf_op jit(solution)/shard_map/reshape | solution.py:164
  1.6 0.8 %reshape.52 = s32[256,8]{1,0:T(8,128)S(1)} reshape(s32[2048]{0:T(1024)} %param.4) | data formatting | bytes 16384 | tf_op jit(solution)/shard_map/reshape | solution.py:165
  2.5 0.7 %gather_fusion = s32[256,8]{1,0:T(8,128)S(1)} fusion(s32[256,8]{1,0:T(8,128)S(1)} %reshape.52, s32[1024]{0:T(1024)S(1)} %pad_clamp_fusion), kind=kCustom, calls=%fused_computation | custom fusion | bytes 17408 | tf_op jit(solution)/shard_map/jit(_take)/gather | solution.py:165
  3.2 0.1 copy.10
  3.2 0.6 %fusion.walk_ref = s32[8,256]{1,0:T(8,128)} fusion(s32[256,8]{0,1:T(8,128)S(1)} %copy.10, pred[256]{0:T(512)(128)(4,1)S(1)} %compare_and_fusion), kind=kLoop, calls=%fused_computation.7 | loop fusion | flops 2048 | bytes 16640 | tf_op jit(solution)/shard_map/jit(_take)/select_n | solution.py:165
  3.9 16.9 %shard_map.37 = f32[8,40,256]{2,1,0:T(8,128)} custom-call(s32[1]{0:T(128)} %bitcast.slow_ref, bf16[8,2,32,2048]{3,2,1,0:T(8,128)(2,1)} %x_ref.1, s32[1,256]{1,0:T(1,128)} %reshape.51.order_ref, s32[8,256]{1,0:T(8,128)} %fusion.walk_ref), custom_call_target="tpu_custom_call" | custom-call | tf_op jit(solution)/shard_map/pallas_call | solution.py:166
  20.7 6.5 %all-to-all-start = ((f32[8,40,256]{2,1,0:T(8,128)}), f32[8,40,256]{2,1,0:T(8,128)S(1)}, u32[]{:S(2)}, u32[]{:S(2)}) async-start(f32[8,40,256]{2,1,0:T(8,128)} %shard_map.37), calls=%async_computation | async-start | bytes 655360 | tf_op jit(solution)/shard_map/all_to_all | solution.py:178
  27.3 0.1 dynamic-slice_bitcast_fusion
  27.4 0.6 %reshape.53.walk_ref = s32[1,256]{1,0:T(1,128)} reshape(s32[8,32]{1,0:T(8,128)S(1)} %dynamic-slice_bitcast_fusion) | data formatting | bytes 2048 | tf_op jit(solution)/shard_map/reshape | solution.py:179
  28.0 6.4 %all-to-all-done.x_ref = f32[8,40,256]{2,1,0:T(8,128)S(1)} async-done(((f32[8,40,256]{2,1,0:T(8,128)}), f32[8,40,256]{2,1,0:T(8,128)S(1)}, u32[]{:S(2)}, u32[]{:S(2)}) %all-to-all-start) | async-done | bytes 327712 | tf_op jit(solution)/shard_map/all_to_all | solution.py:178
  34.4 0.0 copy-start
  34.4 0.7 %copy-done = f32[8,40,256]{2,1,0:T(8,128)} copy-done((f32[8,40,256]{2,1,0:T(8,128)}, f32[8,40,256]{2,1,0:T(8,128)S(1)}, u32[]{:S(2)}) %copy-start) | copy-done | bytes 327704
  35.1 2.2 %shard_map.38 = f32[32,8,128]{2,1,0:T(8,128)} custom-call(f32[8,40,256]{2,1,0:T(8,128)} %copy-done, s32[1,256]{1,0:T(1,128)} %reshape.53.walk_ref), custom_call_target="tpu_custom_call" | custom-call | tf_op jit(solution)/shard_map/pallas_call | solution.py:180
  37.3 20.0 %all_to_all.10.x_ref = f32[32,8,128]{2,1,0:T(8,128)} all-to-all(f32[32,8,128]{2,1,0:T(8,128)} %shard_map.38), channel_id=1, replica_groups=mesh['dop'=32,'slow'=8] {'dop'}, dimensions={0} | all-to-all | bytes 262144 | tf_op jit(solution)/shard_map/all_to_all | solution.py:187
  57.3 1.6 %shard_map.39 = f32[8,1024]{1,0:T(8,128)} custom-call(f32[32,8,128]{2,1,0:T(8,128)} %all_to_all.10.x_ref), custom_call_target="tpu_custom_call" | custom-call | tf_op jit(solution)/shard_map/pallas_call | solution.py:188
  (4 shorter events, 0.0 us)
Async XLA Ops:
  20.7 13.6 %all-to-all-start = ((f32[8,40,256]{2,1,0:T(8,128)}), f32[8,40,256]{2,1,0:T(8,128)S(1)}, u32[]{:S(2)}, u32[]{:S(2)}) async-start(f32[8,40,256]{2,1,0:T(8,128)} %shard_map.37), calls=%async_computation | async-start | bytes 655360 | tf_op jit(solution)/shard_map/all_to_all | solution.py:178
  34.4 0.7 %copy-start = (f32[8,40,256]{2,1,0:T(8,128)}, f32[8,40,256]{2,1,0:T(8,128)S(1)}, u32[]{:S(2)}) copy-start(f32[8,40,256]{2,1,0:T(8,128)S(1)} %all-to-all-done.x_ref) | copy-start | bytes 983044

commit v2 on v0

v2 whole, which is shorter than its diff:
```python
import math

import jax
import jax.numpy as jnp
from jax import lax
from jax.experimental import pallas as pl
from jax.experimental.pallas import tpu as pltpu
from jax.sharding import Mesh, PartitionSpec as P

F = 2048
BANDS = 256
ROWS = 32
PER = 8
WIN = 40
SCALE = 1.0 / (64 * F)
f32 = jnp.float32
bf16 = jnp.bfloat16


def cos_sin(turns, period):
    quarter = period // 4
    shift = quarter.bit_length() - 1
    quad = (turns + quarter // 2) >> shift
    r = (turns - (quad << shift)).astype(f32) * (2.0 * math.pi / period)
    r2 = r * r
    c = 1.0 + r2 * (-1 / 2 + r2 * (1 / 24 + r2 * (-1 / 720 + r2 * (1 / 40320))))
    s = r * (1.0 + r2 * (-1 / 6 + r2 * (1 / 120 + r2 * (-1 / 5040 + r2 * (1 / 362880)))))
    odd = (quad & 1) == 1
    cosine = jnp.where(odd, s, c)
    sine = jnp.where(odd, c, s)
    cosine = jnp.where(((quad + 1) & 2) == 2, -cosine, cosine)
    sine = jnp.where((quad & 2) == 2, -sine, sine)
    return cosine, sine


def iota(shape, dim):
    return lax.broadcasted_iota(jnp.int32, shape, dim)


def spectra_kernel(
    place_ref, x_hbm, order_ref, walk_ref, send_ref, keep_ref, meet_ref,
    x_ref, odd_ref, even_ref, wodd_ref, weven_ref, sems,
):
    slow = place_ref[0]
    core = place_ref[1]
    copies = [pltpu.make_async_copy(x_hbm.at[g], x_ref.at[g], sems.at[g]) for g in range(PER)]
    for copy in copies:
        copy.start()

    order = order_ref[...].astype(f32).astype(bf16)
    halves = []
    for c in range(2):
        owner = ((iota((128, 128), 1) & 31) << 3) + ((iota((128, 128), 1) >> 5) << 1) + c
        pick = iota((128, 128), 0) == (owner & 127)
        got = jnp.dot(order, pick.astype(f32).astype(bf16), preferred_element_type=f32)
        halves.append(jnp.where((iota((1, 128), 1) & 31) < 16, got[0:1], got[1:2]))
    flip = core == 0
    bands = jnp.concatenate(
        [jnp.where(flip, halves[1], halves[0]), jnp.where(flip, halves[0], halves[1])], axis=1
    ).astype(jnp.int32)

    band_cos, band_sin = cos_sin((iota((BANDS, BANDS), 0) * bands) & (BANDS - 1), BANDS)
    fine_cos, fine_sin = cos_sin((iota((512, 128), 0) * (iota((512, 128), 1) & 7)) & (F - 1), F)

    def table(j):
        for half in range(2 if j % 2 else 1):
            at = half * 256
            fc = fine_cos[at : at + 256, j : j + 1]
            fs = fine_sin[at : at + 256, j : j + 1]
            c = (band_cos * fc - band_sin * fs).astype(bf16)
            s = (band_sin * fc + band_cos * fs).astype(bf16)
            if j % 2:
                wodd_ref[j // 2, at : at + 256, :] = c
                wodd_ref[j // 2, 512 + at : 512 + at + 256, :] = s
            else:
                weven_ref[j // 2, 0:256, :] = c
                weven_ref[j // 2, 256:512, :] = s

    def put(ref, index, row, col, depth, zr, zi):
        rh = zr.astype(bf16)
        ih = zi.astype(bf16)
        rl = (zr - rh.astype(f32)).astype(bf16)
        il = (zi - ih.astype(f32)).astype(bf16)
        for level, (re, im) in enumerate(((rh, ih), (rl, il))):
            ref[index, level, row : row + 16, col : col + 128] = re
            ref[index, level, row : row + 16, depth + col : depth + col + 128] = im
            ref[index, level, 256 + row : 256 + row + 16, col : col + 128] = im
            ref[index, level, 256 + row : 256 + row + 16, depth + col : depth + col + 128] = -re

    def fold(g, part, pair):
        zs = []
        for cb in (pair, pair + 2):
            re, im = [
                [
                    x_ref[
                        g, c, part * 16 : part * 16 + 16, k * 512 + cb * 128 : k * 512 + cb * 128 + 128
                    ].astype(f32)
                    for k in range(4)
                ]
                for c in range(2)
            ]
            s02r, s02i = re[0] + re[2], im[0] + im[2]
            d02r, d02i = re[0] - re[2], im[0] - im[2]
            s13r, s13i = re[1] + re[3], im[1] + im[3]
            d13r, d13i = re[1] - re[3], im[1] - im[3]
            row = g * ROWS + part * 16
            put(odd_ref, 0, row, cb * 128, 512, d02r + d13i, d02i - d13r)
            put(odd_ref, 1, row, cb * 128, 512, d02r - d13i, d02i + d13r)
            zs.append((s02r + s13r, s02i + s13i, s02r - s13r, s02i - s13i))
        (ar, ai, cr, ci), (br, bi, dr, di) = zs
        put(even_ref, 0, row, pair * 128, 256, ar + br, ai + bi)
        put(even_ref, 2, row, pair * 128, 256, ar - br, ai - bi)
        put(even_ref, 1, row, pair * 128, 256, cr + di, ci - dr)
        put(even_ref, 3, row, pair * 128, 256, cr - di, ci + dr)

    rows16 = iota((16, BANDS), 0) == (bands >> 4)
    walks = []
    for j in range(8):
        pick = iota((128, BANDS), 0) == (((bands & 15) << 3) + j)
        got = jnp.dot(
            walk_ref[...].astype(f32).astype(bf16),
            pick.astype(f32).astype(bf16),
            preferred_element_type=f32,
        )
        walks.append(jnp.sum(jnp.where(rows16, got, 0.0), axis=0, keepdims=True).astype(jnp.int32))

    def align(j, spec):
        powers = spec[:256] * spec[:256] + spec[256:] * spec[256:]
        walk = walks[j]
        ahead = walk >= 0
        at = [(walk * (8 * slow + g)) >> 6 for g in range(PER)]
        rim = jnp.zeros((WIN - ROWS, BANDS), f32)
        total = None
        for i in range(PER):
            own = jnp.where(
                ahead, powers[i * ROWS : (i + 1) * ROWS], powers[(7 - i) * ROWS : (8 - i) * ROWS]
            )
            own = jnp.concatenate([own, rim], axis=0)
            if i == 0:
                total = own
            else:
                step = jnp.where(ahead, at[i] - at[i - 1], at[7 - i] - at[8 - i]) == 1
                total = jnp.where(step, pltpu.roll(total, 1, 0), total) + own
        send_ref[j] = total[:, :128]
        keep_ref[j] = total[:, 128:]
        meet = walk[:, 128:]
        lower = slow & ~1
        apart = jnp.where(
            meet >= 0,
            ((meet * (8 * lower + 15)) >> 6) - ((meet * (8 * lower + 7)) >> 6),
            ((meet * (8 * lower)) >> 6) - ((meet * (8 * lower + 8)) >> 6),
        )
        meet_ref[j : j + 1, :] = jnp.where(meet >= 0, apart, -apart - 1)

    for j in range(8):
        table(j)
    for g in range(PER):
        copies[g].wait()
        for part in range(2):
            for pair in range(2):
                fold(g, part, pair)

    def product(j):
        if j % 2:
            left, index, w = odd_ref, (j // 2) % 2, wodd_ref[j // 2]
        else:
            left, index, w = even_ref, j // 2, weven_ref[j // 2]
        return jnp.dot(left[index, 0], w, preferred_element_type=f32) + jnp.dot(
            left[index, 1], w, preferred_element_type=f32
        )

    for j in (1, 5, 3, 7, 0, 2, 4, 6):
        align(j, product(j))


def pair_kernel(place_ref, mine_ref, theirs_ref, meet_ref, out_ref, flat_ref):
    first = place_ref[1] == 0
    for j in range(8):
        mine = mine_ref[j]
        theirs = theirs_ref[j]
        lower = jnp.where(first, mine, theirs)
        upper = jnp.where(first, theirs, mine)
        meet = meet_ref[j : j + 1, :]
        ahead = meet >= 0
        apart = jnp.where(ahead, meet, -meet - 1)
        moved = jnp.where(ahead, lower, upper)
        still = jnp.where(ahead, upper, lower)
        for bit in range(3):
            moved = jnp.where(((apart >> bit) & 1) == 1, pltpu.roll(moved, 1 << bit, 0), moved)
        flat_ref[j * WIN : (j + 1) * WIN, :] = moved + still
    flat_ref[8 * WIN :, :] = jnp.zeros((64, 128), f32)
    for piece in range(3):
        part = slice(piece * 128, (piece + 1) * 128)
        out_ref[:, part] = flat_ref[part, :].T


def join_kernel(place_ref, order_ref, walk_ref, x_ref, out_ref, turned_ref):
    owner = place_ref[2]
    band = order_ref[owner]
    lane = iota((1, 128), 1)
    group = lane // 32
    block = lane & 31
    flat = jnp.concatenate(
        [x_ref[:, piece * 128 : (piece + 1) * 128].T for piece in range(3)], axis=0
    )
    for quad in range(2):
        packed = None
        for jq in range(4):
            j = quad * 4 + jq
            walk = walk_ref[band * 8 + j]
            last = jnp.where(walk >= 0, 15, 0)
            move = jnp.zeros((1, 128), jnp.int32)
            for x in range(4):
                move = jnp.where(group == x, 32 - ((walk * (16 * x + last)) >> 6), move)
            current = jnp.concatenate(
                [flat[j * WIN : (j + 1) * WIN], jnp.zeros((8, 128), f32)], axis=0
            )
            for bit in range(6):
                taken = ((move >> bit) & 1) == 1
                if bit < 3:
                    current = jnp.where(taken, pltpu.roll(current, 1 << bit, 0), current)
                else:
                    pad = jnp.zeros((1 << bit, 128), f32)
                    low = jnp.concatenate([current, pad], axis=0)
                    high = jnp.concatenate([pad, current], axis=0)
                    current = jnp.where(taken, high[:96], low[:96])
            current = current + pltpu.roll(current, 64, 1)
            current = current + pltpu.roll(current, 32, 1)
            before = jnp.where(block == 31, 0.0, pltpu.roll(current[0:32], 127, 1))
            after = jnp.where(block == 0, 0.0, pltpu.roll(current[64:96], 1, 1))
            summed = before + current[32:64] + after
            packed = summed if packed is None else jnp.where(group == jq, summed, packed)
        packed = packed * SCALE
        turned_ref[quad * 128 : (quad + 1) * 128, :] = jnp.concatenate([packed] * 4, axis=0).T
    for v in range(8):
        result = None
        for c in range(4):
            piece = turned_ref[pl.ds(4 * v + c, 8, stride=32), :]
            result = piece if result is None else jnp.where(group == c, piece, result)
        out_ref[:, v * 128 : (v + 1) * 128] = result


VM = pl.BlockSpec(memory_space=pltpu.VMEM)
SM = pl.BlockSpec(memory_space=pltpu.SMEM)


def on_device(profiles, range_walk, band_order):
    x, core = lax.axis_index("x"), lax.axis_index("c")
    slow = 2 * x + core
    owner = (lax.axis_index("z") * 4 + lax.axis_index("y")) * 8 + slow
    place = jnp.stack([slow, core, owner]).astype(jnp.int32)
    block = jax.ShapeDtypeStruct((8, WIN, 128), f32)
    send, keep, meet = pl.pallas_call(
        spectra_kernel,
        out_shape=(block, block, jax.ShapeDtypeStruct((8, 128), jnp.int32)),
        in_specs=[SM, pl.BlockSpec(memory_space=pltpu.HBM), VM, VM],
        out_specs=(VM, VM, VM),
        scratch_shapes=[
            pltpu.VMEM((PER, 2, ROWS, F), bf16),
            pltpu.VMEM((2, 2, 512, 1024), bf16),
            pltpu.VMEM((4, 2, 512, 512), bf16),
            pltpu.VMEM((4, 1024, 256), bf16),
            pltpu.VMEM((4, 512, 256), bf16),
            pltpu.SemaphoreType.DMA((PER,)),
        ],
        compiler_params=pltpu.CompilerParams(vmem_limit_bytes=40 << 20),
    )(place, profiles, band_order.reshape(2, 128), range_walk.reshape(16, 128))
    theirs = lax.ppermute(send, "c", [(0, 1), (1, 0)])
    messages = pl.pallas_call(
        pair_kernel,
        out_shape=jax.ShapeDtypeStruct((128, 384), f32),
        in_specs=[SM, VM, VM, VM],
        out_specs=VM,
        scratch_shapes=[pltpu.VMEM((384, 128), f32)],
        compiler_params=pltpu.CompilerParams(vmem_limit_bytes=4 << 20),
    )(place, keep, theirs, meet)
    arrived = lax.all_to_all(
        messages.reshape(128, 1, 384), ("x", "z", "y"), split_axis=0, concat_axis=0, tiled=True
    )
    return pl.pallas_call(
        join_kernel,
        out_shape=jax.ShapeDtypeStruct((8, 1024), f32),
        in_specs=[SM, SM, SM, VM],
        out_specs=VM,
        scratch_shapes=[pltpu.VMEM((256, 128), f32)],
        compiler_params=pltpu.CompilerParams(vmem_limit_bytes=4 << 20),
    )(place, band_order, range_walk, arrived.reshape(128, 384))


def solution(mesh):
    fine = Mesh(mesh.devices.reshape(8, 4, 4, 2), ("z", "y", "x", "c"))
    placed = (P(("x", "c"), None, ("z", "y"), None), P(), P())
    return jax.shard_map(
        on_device, mesh=fine, in_specs=placed, out_specs=P(("z", "y", "x", "c"), None), check_vma=False
    )
```

time: 233 us -> 43.8 us (0.19)
  matrix products: 129 us -> 0 us
  other arithmetic: 48.1 us -> 0.08 us
  Pallas kernels: 0 us -> 10.5 us
  blocking collectives: 33.9 us -> 25.5 us
  waiting for transfers between devices: 7.5 us -> 1.03 us
  local copies, waits for them, and re-layouts: 7.89 us -> 3.18 us
    dot_general x3 -> x0, matrix products: 129 us -> none  [the longest x1 64.4 us: batch_powers(): jnp.dot(stacked, sine_table, preferred_element_type=jnp.float32)]
    select_n x6 -> x0, other arithmetic: 41 us -> none  [walk_align(): current = jnp.where(taken, current[:, stride:], current[:, :-stride])]
    pallas_call x0 -> x3, Pallas kernels: none -> 10.5 us  [the longest x1 7.78 us: on_device(): pl.pallas_call(spectra_kernel, out_shape=(block, block, jax.ShapeDtypeStr...]
    all_to_all x2 -> x1, blocking collectives: 33.9 us -> 25.5 us  [on_device(): lax.all_to_all(messages.reshape(128, 1, 384), ('x', 'z', 'y'), split_axis...]
    ppermute x2 -> x1, waiting for transfers between devices: 7.5 us -> 1.03 us  [on_device(): theirs = lax.ppermute(send, 'c', [(0, 1), (1, 0)])]
    add x2 -> x0, other arithmetic: 4.51 us -> none  [the longest x1 4.51 us: batch_powers(): return real_part * real_part + imag_part * imag_part]
    transpose x3 -> x0, local copies, waits for them, and re-layouts: 3.95 us -> none  [the longest x1 1.53 us: cut_along(): return jnp.moveaxis(x.reshape(*before, devices, -1, *after), dim, 0)]
    ppermute x2 -> x1, starting transfers between devices: 5.33 us -> 3.29 us  [on_device(): theirs = lax.ppermute(send, 'c', [(0, 1), (1, 0)])]
  transfers between devices with their start and end apart: 2 -> 1, of which waited for: 2 -> 1; matrix products, arithmetic and copies ran while one was open for 0% -> 0% of each run, Pallas kernels for 0% -> 0%
where the time goes in v2:
time: 43.8 us; the launch traced here: 43.6 us
  blocking collectives  25.5 us (58%)
  Pallas kernels  10.5 us (24%)
  starting transfers between devices  3.29 us (8%)
  local copies, waits for them, and re-layouts  3.18 us (7%)
  waiting for transfers between devices  1.03 us (2%)
    all_to_all x1, blocking collectives, on_device(): lax.all_to_all(messages.reshape(128, 1, 384), ('x', 'z', 'y'), split_axis...  25.5 us
    pallas_call x1, Pallas kernels, on_device(): pl.pallas_call(spectra_kernel, out_shape=(block, block, jax.ShapeDtypeStr...  7.78 us
    ppermute x1, starting transfers between devices, on_device(): theirs = lax.ppermute(send, 'c', [(0, 1), (1, 0)])  3.29 us
    unnamed x7, local copies, waits for them, and re-layouts  2.98 us
    pallas_call x1, Pallas kernels, on_device(): pl.pallas_call(join_kernel, out_shape=jax.ShapeDtypeStruct((8, 1024), f32...  1.99 us
    ppermute x1, waiting for transfers between devices, on_device(): theirs = lax.ppermute(send, 'c', [(0, 1), (1, 0)])  1.03 us
  transfers between devices with their start and end apart: 1, of which 1 were waited for; matrix products, arithmetic and copies ran while one was open for 0% of the time, Pallas kernels for 0%

profile of v2, /device:TPU:1, one launch (start us, length us, event | category | flops | bytes accessed | tf_op | source)
XLA Modules:
  0.0 43.6 jit_solution(7813057122613014799)
XLA Ops:
  0.0 0.1 pad_add_fusion.place_ref
  0.1 0.0 copy-start
  0.1 1.6 %copy-done = bf16[8,2,32,2048]{3,2,1,0:T(8,128)(2,1)S(1)} copy-done((bf16[8,2,32,2048]{3,2,1,0:T(8,128)(2,1)S(1)}, bf16[8,2,32,2048]{3,2,1,0:T(8,128)(2,1)}, u32[]{:S(2)}) %copy-start) | copy-done | bytes 2097176
  1.7 0.0 copy-start.1
  1.7 0.7 %copy-done.1 = s32[2048]{0:T(1024)S(1)} copy-done((s32[2048]{0:T(1024)S(1)}, s32[2048]{0:T(1024)}, u32[]{:S(2)}) %copy-start.1) | copy-done | bytes 8216
  2.4 0.0 copy-start.2
  2.4 0.7 %copy-done.2 = s32[256]{0:T(256)S(1)} copy-done((s32[256]{0:T(256)S(1)}, s32[256]{0:T(256)}, u32[]{:S(2)}) %copy-start.2) | copy-done | bytes 1048
  3.0 7.8 %shard_map.37 = (f32[8,40,128]{2,1,0:T(8,128)S(1)}, f32[8,40,128]{2,1,0:T(8,128)S(1)}, s32[8,128]{1,0:T(8,128)S(1)}) custom-call(s32[3]{0:T(128)S(1)} %pad_add_fusion.place_ref, bf16[8,2,32,2048]{3,2,1,0:T(8,128)(2,1)S(1)} %copy-done, s32[2,128]{1,0:T(2,128)S(1)} %bitcast.12, s32[16,128]{1,0:T(8,128)S(1)} %bitcast.11), custom_call_target="tpu_custom_call" | custom-call | tf_op jit(solution)/shard_map/pallas_call | solution.py:253
  10.8 3.3 %collective-permute-start = (f32[8,40,128]{2,1,0:T(8,128)S(1)}, f32[8,40,128]{2,1,0:T(8,128)S(1)}, u32[]{:S(2)}, u32[]{:S(2)}) collective-permute-start(f32[8,40,128]{2,1,0:T(8,128)S(1)} %get-tuple-element.9), channel_id=1, source_target_pairs={{0,1},{1,0},{2,3},{3,2},{4,5},{5,4},{6,7},{7,6},{8,9},{9,8},{10,11... | collective-permute-start | bytes 491528 | tf_op jit(solution)/shard_map/ppermute | solution.py:268
  14.1 1.0 %collective-permute-done.theirs_ref = f32[8,40,128]{2,1,0:T(8,128)S(1)} collective-permute-done((f32[8,40,128]{2,1,0:T(8,128)S(1)}, f32[8,40,128]{2,1,0:T(8,128)S(1)}, u32[]{:S(2)}, u32[]{:S(2)}) %collective-permute-start) | collective-permute-done | bytes 163872 | tf_op jit(solution)/shard_map/ppermute | solution.py:268
  15.2 0.7 %shard_map.38 = f32[128,384]{1,0:T(8,128)S(1)} custom-call(s32[3]{0:T(128)S(1)} %pad_add_fusion.place_ref, f32[8,40,128]{2,1,0:T(8,128)S(1)} %get-tuple-element.8.mine_ref, f32[8,40,128]{2,1,0:T(8,128)S(1)} %collective-permute-done.theirs_ref, s32[8,128]{1,0:T(8,128)S(1)} %get-tuple-element.10.meet_ref), custom_call_target="tpu_custom_call" | custom-call | tf_op jit(solution)/shard_map/pallas_call | solution.py:269
  15.9 0.2 copy.4
  16.1 25.5 %all_to_all.5 = f32[128,1,384]{2,1,0:T(1,128)S(1)} all-to-all(f32[128,1,384]{2,1,0:T(1,128)S(1)} %copy.4), channel_id=1, replica_groups=mesh['z'=8,'y'=4,'x'=4,'c'=2] {'x','z','y'}, dimensions={0} | all-to-all | bytes 393216 | tf_op jit(solution)/shard_map/all_to_all | solution.py:277
  41.6 2.0 %shard_map.39 = f32[8,1024]{1,0:T(8,128)} custom-call(s32[3]{0:T(128)S(1)} %pad_add_fusion.place_ref, s32[256]{0:T(256)S(1)} %copy-done.2, s32[2048]{0:T(1024)S(1)} %copy-done.1, f32[128,384]{1,0:T(8,128)S(1)} %bitcast.10), custom_call_target="tpu_custom_call" | custom-call | tf_op jit(solution)/shard_map/pallas_call | solution.py:280
  (1 shorter events, 0.0 us)
Async XLA Ops:
  0.1 1.6 %copy-start = (bf16[8,2,32,2048]{3,2,1,0:T(8,128)(2,1)S(1)}, bf16[8,2,32,2048]{3,2,1,0:T(8,128)(2,1)}, u32[]{:S(2)}) copy-start(bf16[8,2,32,2048]{3,2,1,0:T(8,128)(2,1)} %x_hbm.1) | copy-start | bytes 6291460
  1.7 0.7 %copy-start.1 = (s32[2048]{0:T(1024)S(1)}, s32[2048]{0:T(1024)}, u32[]{:S(2)}) copy-start(s32[2048]{0:T(1024)} %walk_ref.1) | copy-start | bytes 24580
  2.4 0.7 %copy-start.2 = (s32[256]{0:T(256)S(1)}, s32[256]{0:T(256)}, u32[]{:S(2)}) copy-start(s32[256]{0:T(256)} %order_ref.1) | copy-start | bytes 3076
  10.8 4.3 %collective-permute-start = (f32[8,40,128]{2,1,0:T(8,128)S(1)}, f32[8,40,128]{2,1,0:T(8,128)S(1)}, u32[]{:S(2)}, u32[]{:S(2)}) collective-permute-start(f32[8,40,128]{2,1,0:T(8,128)S(1)} %get-tuple-element.9), channel_id=1, source_target_pairs={{0,1},{1,0},{2,3},{3,2},{4,5},{5,4},{6,7},{7,6},{8,9},{9,8},{10,11... | collective-permute-start | bytes 491528 | tf_op jit(solution)/shard_map/ppermute | solution.py:268

commit v3 on v2

--- a/solution.py
+++ b/solution.py
@@ -12,6 +12,7 @@
 ROWS = 32
 PER = 8
 WIN = 40
+GRANT = 40 << 20
 SCALE = 1.0 / (64 * F)
 f32 = jnp.float32
 bf16 = jnp.bfloat16
@@ -37,16 +38,49 @@
     return lax.broadcasted_iota(jnp.int32, shape, dim)
 
 
+def places():
+    core = lax.axis_index("c")
+    return 2 * lax.axis_index("x") + core, core
+
+
 def spectra_kernel(
-    place_ref, x_hbm, order_ref, walk_ref, send_ref, keep_ref, meet_ref,
-    x_ref, odd_ref, even_ref, wodd_ref, weven_ref, sems,
+    x_hbm, order_hbm, walk_hbm, send_ref, keep_ref, meet_ref, own_ref,
+    x_ref, order_ref, walk_ref, band_ref, fine_ref, sems,
 ):
-    slow = place_ref[0]
-    core = place_ref[1]
-    copies = [pltpu.make_async_copy(x_hbm.at[g], x_ref.at[g], sems.at[g]) for g in range(PER)]
+    copies = [
+        pltpu.make_async_copy(order_hbm, order_ref, sems.at[0]),
+        pltpu.make_async_copy(walk_hbm, walk_ref, sems.at[1]),
+    ]
+    copies += [
+        pltpu.make_async_copy(x_hbm.at[g], x_ref.at[g], sems.at[2 + g]) for g in range(PER)
+    ]
     for copy in copies:
         copy.start()
-
+    packed = lambda *shape: pltpu.VMEM(shape, bf16)
+    pl.run_scoped(
+        lambda *refs: spectra(
+            copies, send_ref, keep_ref, meet_ref, own_ref,
+            x_ref, order_ref, walk_ref, band_ref, fine_ref, *refs
+        ),
+        packed(2, 2, 512, 1024),
+        packed(4, 2, 512, 512),
+        packed(4, 1024, 256),
+        packed(4, 512, 256),
+    )
+
+
+def spectra(
+    copies, send_ref, keep_ref, meet_ref, own_ref,
+    x_ref, order_ref, walk_ref, band_ref, fine_ref,
+    odd_ref, even_ref, wodd_ref, weven_ref,
+):
+    slow, core = places()
+    for at in range(0, 512, 32):
+        fine = cos_sin(((iota((32, 128), 0) + at) * (iota((32, 128), 1) & 7)) & (F - 1), F)
+        fine_ref[0, at : at + 32, :] = fine[0]
+        fine_ref[1, at : at + 32, :] = fine[1]
+
+    copies[0].wait()
     order = order_ref[...].astype(f32).astype(bf16)
     halves = []
     for c in range(2):
@@ -59,22 +93,28 @@
         [jnp.where(flip, halves[1], halves[0]), jnp.where(flip, halves[0], halves[1])], axis=1
     ).astype(jnp.int32)
 
-    band_cos, band_sin = cos_sin((iota((BANDS, BANDS), 0) * bands) & (BANDS - 1), BANDS)
-    fine_cos, fine_sin = cos_sin((iota((512, 128), 0) * (iota((512, 128), 1) & 7)) & (F - 1), F)
+    for at in range(0, BANDS, 16):
+        turns = ((iota((16, BANDS), 0) + at) * bands) & (BANDS - 1)
+        band = cos_sin(turns, BANDS)
+        band_ref[0, at : at + 16, :] = band[0]
+        band_ref[1, at : at + 16, :] = band[1]
 
     def table(j):
         for half in range(2 if j % 2 else 1):
-            at = half * 256
-            fc = fine_cos[at : at + 256, j : j + 1]
-            fs = fine_sin[at : at + 256, j : j + 1]
-            c = (band_cos * fc - band_sin * fs).astype(bf16)
-            s = (band_sin * fc + band_cos * fs).astype(bf16)
-            if j % 2:
-                wodd_ref[j // 2, at : at + 256, :] = c
-                wodd_ref[j // 2, 512 + at : 512 + at + 256, :] = s
-            else:
-                weven_ref[j // 2, 0:256, :] = c
-                weven_ref[j // 2, 256:512, :] = s
+            for row in range(0, 256, 16):
+                at = half * 256 + row
+                fc = fine_ref[0, at : at + 16, j : j + 1]
+                fs = fine_ref[1, at : at + 16, j : j + 1]
+                bc = band_ref[0, row : row + 16, :]
+                bs = band_ref[1, row : row + 16, :]
+                c = (bc * fc - bs * fs).astype(bf16)
+                s = (bs * fc + bc * fs).astype(bf16)
+                if j % 2:
+                    wodd_ref[j // 2, at : at + 16, :] = c
+                    wodd_ref[j // 2, 512 + at : 512 + at + 16, :] = s
+                else:
+                    weven_ref[j // 2, at : at + 16, :] = c
+                    weven_ref[j // 2, 256 + at : 256 + at + 16, :] = s
 
     def put(ref, index, row, col, depth, zr, zi):
         rh = zr.astype(bf16)
@@ -87,46 +127,57 @@
             ref[index, level, 256 + row : 256 + row + 16, col : col + 128] = im
             ref[index, level, 256 + row : 256 + row + 16, depth + col : depth + col + 128] = -re
 
-    def fold(g, part, pair):
+    def quarters(g, part, cb):
+        return [
+            [
+                x_ref[
+                    g, c, part * 16 : part * 16 + 16, k * 512 + cb * 128 : k * 512 + cb * 128 + 128
+                ].astype(f32)
+                for k in range(4)
+            ]
+            for c in range(2)
+        ]
+
+    def fold_odd(g, part, cb):
+        re, im = quarters(g, part, cb)
+        dr, di = re[0] - re[2], im[0] - im[2]
+        er, ei = re[1] - re[3], im[1] - im[3]
+        row = g * ROWS + part * 16
+        put(odd_ref, 0, row, cb * 128, 512, dr + ei, di - er)
+        put(odd_ref, 1, row, cb * 128, 512, dr - ei, di + er)
+
+    def fold_even(g, part, pair):
+        row = g * ROWS + part * 16
         zs = []
         for cb in (pair, pair + 2):
-            re, im = [
-                [
-                    x_ref[
-                        g, c, part * 16 : part * 16 + 16, k * 512 + cb * 128 : k * 512 + cb * 128 + 128
-                    ].astype(f32)
-                    for k in range(4)
-                ]
-                for c in range(2)
-            ]
-            s02r, s02i = re[0] + re[2], im[0] + im[2]
-            d02r, d02i = re[0] - re[2], im[0] - im[2]
-            s13r, s13i = re[1] + re[3], im[1] + im[3]
-            d13r, d13i = re[1] - re[3], im[1] - im[3]
-            row = g * ROWS + part * 16
-            put(odd_ref, 0, row, cb * 128, 512, d02r + d13i, d02i - d13r)
-            put(odd_ref, 1, row, cb * 128, 512, d02r - d13i, d02i + d13r)
-            zs.append((s02r + s13r, s02i + s13i, s02r - s13r, s02i - s13i))
+            re, im = quarters(g, part, cb)
+            sr, si = re[0] + re[2], im[0] + im[2]
+            ur, ui = re[1] + re[3], im[1] + im[3]
+            zs.append((sr + ur, si + ui, sr - ur, si - ui))
         (ar, ai, cr, ci), (br, bi, dr, di) = zs
         put(even_ref, 0, row, pair * 128, 256, ar + br, ai + bi)
         put(even_ref, 2, row, pair * 128, 256, ar - br, ai - bi)
         put(even_ref, 1, row, pair * 128, 256, cr + di, ci - dr)
         put(even_ref, 3, row, pair * 128, 256, cr - di, ci + dr)
 
-    rows16 = iota((16, BANDS), 0) == (bands >> 4)
-    walks = []
-    for j in range(8):
-        pick = iota((128, BANDS), 0) == (((bands & 15) << 3) + j)
-        got = jnp.dot(
-            walk_ref[...].astype(f32).astype(bf16),
-            pick.astype(f32).astype(bf16),
-            preferred_element_type=f32,
-        )
-        walks.append(jnp.sum(jnp.where(rows16, got, 0.0), axis=0, keepdims=True).astype(jnp.int32))
-
-    def align(j, spec):
+    def walks_of():
+        copies[1].wait()
+        rows16 = iota((16, BANDS), 0) == (bands >> 4)
+        walks = []
+        for j in range(8):
+            pick = iota((128, BANDS), 0) == (((bands & 15) << 3) + j)
+            got = jnp.dot(
+                walk_ref[...].astype(f32).astype(bf16),
+                pick.astype(f32).astype(bf16),
+                preferred_element_type=f32,
+            )
+            walk = jnp.sum(jnp.where(rows16, got, 0.0), axis=0, keepdims=True).astype(jnp.int32)
+            own_ref[j : j + 1, :] = walk[:, 128:]
+            walks.append(walk)
+        return walks
+
+    def align(j, walk, spec):
         powers = spec[:256] * spec[:256] + spec[256:] * spec[256:]
-        walk = walks[j]
         ahead = walk >= 0
         at = [(walk * (8 * slow + g)) >> 6 for g in range(PER)]
         rim = jnp.zeros((WIN - ROWS, BANDS), f32)
@@ -152,14 +203,6 @@
         )
         meet_ref[j : j + 1, :] = jnp.where(meet >= 0, apart, -apart - 1)
 
-    for j in range(8):
-        table(j)
-    for g in range(PER):
-        copies[g].wait()
-        for part in range(2):
-            for pair in range(2):
-                fold(g, part, pair)
-
     def product(j):
         if j % 2:
             left, index, w = odd_ref, (j // 2) % 2, wodd_ref[j // 2]
@@ -169,12 +212,26 @@
             left[index, 1], w, preferred_element_type=f32
         )
 
+    walks = walks_of()
     for j in (1, 5, 3, 7, 0, 2, 4, 6):
-        align(j, product(j))
-
-
-def pair_kernel(place_ref, mine_ref, theirs_ref, meet_ref, out_ref, flat_ref):
-    first = place_ref[1] == 0
+        table(j)
+    for g in range(PER):
+        copies[2 + g].wait()
+        for part in range(2):
+            for cb in range(4):
+                fold_odd(g, part, cb)
+    for j in (1, 5):
+        align(j, walks[j], product(j))
+    for g in range(PER):
+        for part in range(2):
+            for pair in range(2):
+                fold_even(g, part, pair)
+    for j in (3, 7, 0, 2, 4, 6):
+        align(j, walks[j], product(j))
+
+
+def pair_kernel(mine_ref, theirs_ref, meet_ref, out_ref, flat_ref):
+    first = lax.axis_index("c") == 0
     for j in range(8):
         mine = mine_ref[j]
         theirs = theirs_ref[j]
@@ -194,12 +251,14 @@
         out_ref[:, part] = flat_ref[part, :].T
 
 
-def join_kernel(place_ref, order_ref, walk_ref, x_ref, out_ref, turned_ref):
-    owner = place_ref[2]
-    band = order_ref[owner]
+def join_kernel(walk_ref, x_ref, out_ref, turned_ref):
     lane = iota((1, 128), 1)
     group = lane // 32
     block = lane & 31
+    here = lax.axis_index("x") * 32 + lax.axis_index("z") * 4 + lax.axis_index("y")
+    walk = jnp.sum(jnp.where(lane == here, walk_ref[...], 0), axis=1, keepdims=True)
+    batch = 16 * group + jnp.where(walk >= 0, 15, 0)
+    moves = 32 - ((walk * batch) >> 6)
     flat = jnp.concatenate(
         [x_ref[:, piece * 128 : (piece + 1) * 128].T for piece in range(3)], axis=0
     )
@@ -207,11 +266,7 @@
         packed = None
         for jq in range(4):
             j = quad * 4 + jq
-            walk = walk_ref[band * 8 + j]
-            last = jnp.where(walk >= 0, 15, 0)
-            move = jnp.zeros((1, 128), jnp.int32)
-            for x in range(4):
-                move = jnp.where(group == x, 32 - ((walk * (16 * x + last)) >> 6), move)
+            move = moves[j : j + 1, :]
             current = jnp.concatenate(
                 [flat[j * WIN : (j + 1) * WIN], jnp.zeros((8, 128), f32)], axis=0
             )
@@ -241,50 +296,52 @@
 
 
 VM = pl.BlockSpec(memory_space=pltpu.VMEM)
-SM = pl.BlockSpec(memory_space=pltpu.SMEM)
 
 
 def on_device(profiles, range_walk, band_order):
-    x, core = lax.axis_index("x"), lax.axis_index("c")
-    slow = 2 * x + core
-    owner = (lax.axis_index("z") * 4 + lax.axis_index("y")) * 8 + slow
-    place = jnp.stack([slow, core, owner]).astype(jnp.int32)
     block = jax.ShapeDtypeStruct((8, WIN, 128), f32)
-    send, keep, meet = pl.pallas_call(
+    row = jax.ShapeDtypeStruct((8, 128), jnp.int32)
+    ANY = pl.BlockSpec(memory_space=pltpu.HBM)
+    send, keep, meet, walks = pl.pallas_call(
         spectra_kernel,
-        out_shape=(block, block, jax.ShapeDtypeStruct((8, 128), jnp.int32)),
-        in_specs=[SM, pl.BlockSpec(memory_space=pltpu.HBM), VM, VM],
-        out_specs=(VM, VM, VM),
+        out_shape=(block, block, row, row),
+        in_specs=[ANY, ANY, ANY],
+        out_specs=(VM, VM, VM, VM),
         scratch_shapes=[
             pltpu.VMEM((PER, 2, ROWS, F), bf16),
-            pltpu.VMEM((2, 2, 512, 1024), bf16),
-            pltpu.VMEM((4, 2, 512, 512), bf16),
-            pltpu.VMEM((4, 1024, 256), bf16),
-            pltpu.VMEM((4, 512, 256), bf16),
-            pltpu.SemaphoreType.DMA((PER,)),
+            pltpu.VMEM((2, 128), jnp.int32),
+            pltpu.VMEM((16, 128), jnp.int32),
+            pltpu.VMEM((2, BANDS, BANDS), f32),
+            pltpu.VMEM((2, 512, 128), f32),
+            pltpu.SemaphoreType.DMA((2 + PER,)),
         ],
-        compiler_params=pltpu.CompilerParams(vmem_limit_bytes=40 << 20),
-    )(place, profiles, band_order.reshape(2, 128), range_walk.reshape(16, 128))
+        compiler_params=pltpu.CompilerParams(vmem_limit_bytes=GRANT),
+    )(
+        *(
+            pltpu.with_memory_space_constraint(array, pltpu.HBM)
+            for array in (profiles, band_order.reshape(2, 128), range_walk.reshape(16, 128))
+        )
+    )
     theirs = lax.ppermute(send, "c", [(0, 1), (1, 0)])
     messages = pl.pallas_call(
         pair_kernel,
         out_shape=jax.ShapeDtypeStruct((128, 384), f32),
-        in_specs=[SM, VM, VM, VM],
+        in_specs=[VM, VM, VM],
         out_specs=VM,
         scratch_shapes=[pltpu.VMEM((384, 128), f32)],
         compiler_params=pltpu.CompilerParams(vmem_limit_bytes=4 << 20),
-    )(place, keep, theirs, meet)
+    )(keep, theirs, meet)
     arrived = lax.all_to_all(
         messages.reshape(128, 1, 384), ("x", "z", "y"), split_axis=0, concat_axis=0, tiled=True
     )
     return pl.pallas_call(
         join_kernel,
         out_shape=jax.ShapeDtypeStruct((8, 1024), f32),
-        in_specs=[SM, SM, SM, VM],
+        in_specs=[VM, VM],
         out_specs=VM,
         scratch_shapes=[pltpu.VMEM((256, 128), f32)],
         compiler_params=pltpu.CompilerParams(vmem_limit_bytes=4 << 20),
-    )(place, band_order, range_walk, arrived.reshape(128, 384))
+    )(walks, arrived.reshape(128, 384))
 
 
 def solution(mesh):

time: 43.8 us -> 38.7 us (0.88)
  local copies, waits for them, and re-layouts: 3.18 us -> 0.22 us
  Pallas kernels: 10.5 us -> 8.53 us
    unnamed x7 -> x1, local copies, waits for them, and re-layouts: 2.98 us -> 0.01 us
    pallas_call x1, Pallas kernels: 7.78 us -> 6.95 us  [on_device(): pl.pallas_call(spectra_kernel, out_shape=(block, block, row, row), in_spe...]
    pallas_call x1, Pallas kernels: 1.99 us -> 1.39 us  [on_device(): pl.pallas_call(join_kernel, out_shape=jax.ShapeDtypeStruct((8, 1024), f32...]
    pallas_call x1, Pallas kernels: 0.72 us -> 0.19 us  [on_device(): pl.pallas_call(pair_kernel, out_shape=jax.ShapeDtypeStruct((128, 384), f3...]
where the time goes in v3:
time: 38.7 us; the launch traced here: 38.6 us
  blocking collectives  25.5 us (66%)
  Pallas kernels  8.53 us (22%)
  starting transfers between devices  3.29 us (9%)
  waiting for transfers between devices  1.03 us (3%)
    all_to_all x1, blocking collectives, on_device(): lax.all_to_all(messages.reshape(128, 1, 384), ('x', 'z', 'y'), split_axis...  25.5 us
    pallas_call x1, Pallas kernels, on_device(): pl.pallas_call(spectra_kernel, out_shape=(block, block, row, row), in_spe...  6.95 us
    ppermute x1, starting transfers between devices, on_device(): theirs = lax.ppermute(send, 'c', [(0, 1), (1, 0)])  3.29 us
    pallas_call x1, Pallas kernels, on_device(): pl.pallas_call(join_kernel, out_shape=jax.ShapeDtypeStruct((8, 1024), f32...  1.39 us
    ppermute x1, waiting for transfers between devices, on_device(): theirs = lax.ppermute(send, 'c', [(0, 1), (1, 0)])  1.03 us
  transfers between devices with their start and end apart: 1, of which 1 were waited for; matrix products, arithmetic and copies ran while one was open for 0% of the time, Pallas kernels for 0%

profile of v3, /device:TPU:1, one launch (start us, length us, event | category | flops | bytes accessed | tf_op | source)
XLA Modules:
  0.0 38.6 jit_solution(1709952092175886013)
XLA Ops:
  0.0 7.0 %shard_map.37 = (f32[8,40,128]{2,1,0:T(8,128)S(1)}, f32[8,40,128]{2,1,0:T(8,128)S(1)}, s32[8,128]{1,0:T(8,128)S(1)}, s32[8,128]{1,0:T(8,128)S(1)}) custom-call(bf16[8,2,32,2048]{3,2,1,0:T(8,128)(2,1)} %x_hbm.1, s32[2,128]{1,0:T(2,128)} %bitcast.9, s32[16,128]{1,0:T(8,128)} %bitcast.8), custom_call_target="tpu_custom_call" | custom-call | tf_op jit(solution)/shard_map/pallas_call | solution.py:305
  7.0 3.3 %collective-permute-start = (f32[8,40,128]{2,1,0:T(8,128)S(1)}, f32[8,40,128]{2,1,0:T(8,128)S(1)}, u32[]{:S(2)}, u32[]{:S(2)}) collective-permute-start(f32[8,40,128]{2,1,0:T(8,128)S(1)} %get-tuple-element.11), channel_id=1, source_target_pairs={{0,1},{1,0},{2,3},{3,2},{4,5},{5,4},{6,7},{7,6},{8,9},{9,8},{10,11... | collective-permute-start | bytes 491528 | tf_op jit(solution)/shard_map/ppermute | solution.py:325
  10.2 1.0 %collective-permute-done.theirs_ref = f32[8,40,128]{2,1,0:T(8,128)S(1)} collective-permute-done((f32[8,40,128]{2,1,0:T(8,128)S(1)}, f32[8,40,128]{2,1,0:T(8,128)S(1)}, u32[]{:S(2)}, u32[]{:S(2)}) %collective-permute-start) | collective-permute-done | bytes 163872 | tf_op jit(solution)/shard_map/ppermute | solution.py:325
  11.3 0.2 shard_map.38
  11.5 0.2 copy.4
  11.7 25.5 %all_to_all.5 = f32[128,1,384]{2,1,0:T(1,128)S(1)} all-to-all(f32[128,1,384]{2,1,0:T(1,128)S(1)} %copy.4), channel_id=1, replica_groups=mesh['z'=8,'y'=4,'x'=4,'c'=2] {'x','z','y'}, dimensions={0} | all-to-all | bytes 393216 | tf_op jit(solution)/shard_map/all_to_all | solution.py:334
  37.2 1.4 %shard_map.39 = f32[8,1024]{1,0:T(8,128)} custom-call(s32[8,128]{1,0:T(8,128)S(1)} %get-tuple-element.9.walk_ref, f32[128,384]{1,0:T(8,128)S(1)} %bitcast.7), custom_call_target="tpu_custom_call" | custom-call | tf_op jit(solution)/shard_map/pallas_call | solution.py:337
  (1 shorter events, 0.0 us)
Async XLA Ops:
  7.0 4.3 %collective-permute-start = (f32[8,40,128]{2,1,0:T(8,128)S(1)}, f32[8,40,128]{2,1,0:T(8,128)S(1)}, u32[]{:S(2)}, u32[]{:S(2)}) collective-permute-start(f32[8,40,128]{2,1,0:T(8,128)S(1)} %get-tuple-element.11), channel_id=1, source_target_pairs={{0,1},{1,0},{2,3},{3,2},{4,5},{5,4},{6,7},{7,6},{8,9},{9,8},{10,11... | collective-permute-start | bytes 491528 | tf_op jit(solution)/shard_map/ppermute | solution.py:325

commit v4 on v3

--- a/solution.py
+++ b/solution.py
@@ -45,7 +45,7 @@
 
 def spectra_kernel(
     x_hbm, order_hbm, walk_hbm, send_ref, keep_ref, meet_ref, own_ref,
-    x_ref, order_ref, walk_ref, band_ref, fine_ref, sems,
+    x_ref, order_ref, walk_ref, band_ref, fine_ref, power_ref, sems,
 ):
     copies = [
         pltpu.make_async_copy(order_hbm, order_ref, sems.at[0]),
@@ -60,7 +60,7 @@
     pl.run_scoped(
         lambda *refs: spectra(
             copies, send_ref, keep_ref, meet_ref, own_ref,
-            x_ref, order_ref, walk_ref, band_ref, fine_ref, *refs
+            x_ref, order_ref, walk_ref, band_ref, fine_ref, power_ref, *refs
         ),
         packed(2, 2, 512, 1024),
         packed(4, 2, 512, 512),
@@ -71,7 +71,7 @@
 
 def spectra(
     copies, send_ref, keep_ref, meet_ref, own_ref,
-    x_ref, order_ref, walk_ref, band_ref, fine_ref,
+    x_ref, order_ref, walk_ref, band_ref, fine_ref, power_ref,
     odd_ref, even_ref, wodd_ref, weven_ref,
 ):
     slow, core = places()
@@ -99,22 +99,20 @@
         band_ref[0, at : at + 16, :] = band[0]
         band_ref[1, at : at + 16, :] = band[1]
 
-    def table(j):
-        for half in range(2 if j % 2 else 1):
-            for row in range(0, 256, 16):
-                at = half * 256 + row
-                fc = fine_ref[0, at : at + 16, j : j + 1]
-                fs = fine_ref[1, at : at + 16, j : j + 1]
-                bc = band_ref[0, row : row + 16, :]
-                bs = band_ref[1, row : row + 16, :]
-                c = (bc * fc - bs * fs).astype(bf16)
-                s = (bs * fc + bc * fs).astype(bf16)
-                if j % 2:
-                    wodd_ref[j // 2, at : at + 16, :] = c
-                    wodd_ref[j // 2, 512 + at : 512 + at + 16, :] = s
-                else:
-                    weven_ref[j // 2, at : at + 16, :] = c
-                    weven_ref[j // 2, 256 + at : 256 + at + 16, :] = s
+    def table(j, half, row):
+        at = half * 256 + row
+        fc = fine_ref[0, at : at + 16, j : j + 1]
+        fs = fine_ref[1, at : at + 16, j : j + 1]
+        bc = band_ref[0, row : row + 16, :]
+        bs = band_ref[1, row : row + 16, :]
+        c = (bc * fc - bs * fs).astype(bf16)
+        s = (bs * fc + bc * fs).astype(bf16)
+        if j % 2:
+            wodd_ref[j // 2, at : at + 16, :] = c
+            wodd_ref[j // 2, 512 + at : 512 + at + 16, :] = s
+        else:
+            weven_ref[j // 2, at : at + 16, :] = c
+            weven_ref[j // 2, 256 + at : 256 + at + 16, :] = s
 
     def put(ref, index, row, col, depth, zr, zi):
         rh = zr.astype(bf16)
@@ -176,15 +174,18 @@
             walks.append(walk)
         return walks
 
-    def align(j, walk, spec):
-        powers = spec[:256] * spec[:256] + spec[256:] * spec[256:]
+    def align(j, tile):
+        lanes = slice(tile * 128, tile * 128 + 128)
+        walk = walks[j][:, lanes]
         ahead = walk >= 0
         at = [(walk * (8 * slow + g)) >> 6 for g in range(PER)]
-        rim = jnp.zeros((WIN - ROWS, BANDS), f32)
+        rim = jnp.zeros((WIN - ROWS, 128), f32)
         total = None
         for i in range(PER):
             own = jnp.where(
-                ahead, powers[i * ROWS : (i + 1) * ROWS], powers[(7 - i) * ROWS : (8 - i) * ROWS]
+                ahead,
+                power_ref[j, i * ROWS : (i + 1) * ROWS, lanes],
+                power_ref[j, (7 - i) * ROWS : (8 - i) * ROWS, lanes],
             )
             own = jnp.concatenate([own, rim], axis=0)
             if i == 0:
@@ -192,42 +193,78 @@
             else:
                 step = jnp.where(ahead, at[i] - at[i - 1], at[7 - i] - at[8 - i]) == 1
                 total = jnp.where(step, pltpu.roll(total, 1, 0), total) + own
-        send_ref[j] = total[:, :128]
-        keep_ref[j] = total[:, 128:]
-        meet = walk[:, 128:]
+        if tile == 0:
+            send_ref[j] = total
+            return
+        keep_ref[j] = total
         lower = slow & ~1
         apart = jnp.where(
-            meet >= 0,
-            ((meet * (8 * lower + 15)) >> 6) - ((meet * (8 * lower + 7)) >> 6),
-            ((meet * (8 * lower)) >> 6) - ((meet * (8 * lower + 8)) >> 6),
+            ahead,
+            ((walk * (8 * lower + 15)) >> 6) - ((walk * (8 * lower + 7)) >> 6),
+            ((walk * (8 * lower)) >> 6) - ((walk * (8 * lower + 8)) >> 6),
         )
-        meet_ref[j : j + 1, :] = jnp.where(meet >= 0, apart, -apart - 1)
-
-    def product(j):
-        if j % 2:
-            left, index, w = odd_ref, (j // 2) % 2, wodd_ref[j // 2]
-        else:
-            left, index, w = even_ref, j // 2, weven_ref[j // 2]
-        return jnp.dot(left[index, 0], w, preferred_element_type=f32) + jnp.dot(
-            left[index, 1], w, preferred_element_type=f32
-        )
-
+        meet_ref[j : j + 1, :] = jnp.where(ahead, apart, -apart - 1)
+
+    def products(pair, count, at, side):
+        depth = 1024 if pair[0] % 2 else 512
+        sums = [None, None]
+        for level in range(2):
+            for k in range(0, depth, 256):
+                for place, j in enumerate(pair):
+                    if j % 2:
+                        left, index, w = odd_ref, (j // 2) % 2, wodd_ref[j // 2, k : k + 256]
+                    else:
+                        left, index, w = even_ref, j // 2, weven_ref[j // 2, k : k + 256]
+                    rows = jnp.concatenate(
+                        [
+                            left[index, level, at : at + count, k : k + 256],
+                            left[index, level, 256 + at : 256 + at + count, k : k + 256],
+                        ],
+                        axis=0,
+                    )
+                    got = jnp.dot(rows, w, preferred_element_type=f32)
+                    sums[place] = got if sums[place] is None else sums[place] + got
+                share = -(-len(side) // (2 * depth // 256 - level * (depth // 256) - k // 256))
+                for task in side[:share]:
+                    task()
+                side = side[share:]
+        for place, j in enumerate(pair):
+            re, im = sums[place][:count], sums[place][count:]
+            power_ref[j, at : at + count, :] = re * re + im * im
+
+    def later(task, *args):
+        return lambda: task(*args)
+
+    def folds(task, batches, cuts):
+        return [later(task, g, p, c) for g in batches for p in range(2) for c in range(cuts)]
+
+    def aligns(*bins):
+        return [later(align, j, tile) for j in bins for tile in range(2)]
+
+    def tables(*bins):
+        return [
+            later(table, j, half, row)
+            for j in bins
+            for half in range(2 if j % 2 else 1)
+            for row in range(0, 256, 16)
+        ]
+
+    for task in tables(1, 5):
+        task()
     walks = walks_of()
-    for j in (1, 5, 3, 7, 0, 2, 4, 6):
-        table(j)
-    for g in range(PER):
+    for g in range(4):
         copies[2 + g].wait()
-        for part in range(2):
-            for cb in range(4):
-                fold_odd(g, part, cb)
-    for j in (1, 5):
-        align(j, walks[j], product(j))
-    for g in range(PER):
-        for part in range(2):
-            for pair in range(2):
-                fold_even(g, part, pair)
-    for j in (3, 7, 0, 2, 4, 6):
-        align(j, walks[j], product(j))
+    for task in folds(fold_odd, range(4), 4):
+        task()
+    for g in range(4, 8):
+        copies[2 + g].wait()
+    products((1, 5), 128, 0, folds(fold_odd, range(4, 8), 4) + tables(3, 7))
+    products((1, 5), 128, 128, folds(fold_even, range(4), 2) + tables(0, 4))
+    products((3, 7), 256, 0, folds(fold_even, range(4, 8), 2) + tables(2, 6) + aligns(1, 5))
+    products((0, 4), 256, 0, aligns(3, 7))
+    products((2, 6), 256, 0, aligns(0, 4))
+    for task in aligns(2, 6):
+        task()
 
 
 def pair_kernel(mine_ref, theirs_ref, meet_ref, out_ref, flat_ref):
@@ -313,6 +350,7 @@
             pltpu.VMEM((16, 128), jnp.int32),
             pltpu.VMEM((2, BANDS, BANDS), f32),
             pltpu.VMEM((2, 512, 128), f32),
+            pltpu.VMEM((8, 256, 256), f32),
             pltpu.SemaphoreType.DMA((2 + PER,)),
         ],
         compiler_params=pltpu.CompilerParams(vmem_limit_bytes=GRANT),

time: 38.7 us -> 38.2 us (0.987)
  Pallas kernels: 8.53 us -> 8.04 us
    pallas_call x1, Pallas kernels: 6.95 us -> 6.46 us  [on_device(): pl.pallas_call(spectra_kernel, out_shape=(block, block, row, row), in_spe...]
where the time goes in v4:
time: 38.2 us; the launch traced here: 38.1 us
  blocking collectives  25.5 us (67%)
  Pallas kernels  8.04 us (21%)
  starting transfers between devices  3.29 us (9%)
  waiting for transfers between devices  1.03 us (3%)
    all_to_all x1, blocking collectives, on_device(): lax.all_to_all(messages.reshape(128, 1, 384), ('x', 'z', 'y'), split_axis...  25.5 us
    pallas_call x1, Pallas kernels, on_device(): pl.pallas_call(spectra_kernel, out_shape=(block, block, row, row), in_spe...  6.46 us
    ppermute x1, starting transfers between devices, on_device(): theirs = lax.ppermute(send, 'c', [(0, 1), (1, 0)])  3.29 us
    pallas_call x1, Pallas kernels, on_device(): pl.pallas_call(join_kernel, out_shape=jax.ShapeDtypeStruct((8, 1024), f32...  1.39 us
    ppermute x1, waiting for transfers between devices, on_device(): theirs = lax.ppermute(send, 'c', [(0, 1), (1, 0)])  1.03 us
  transfers between devices with their start and end apart: 1, of which 1 were waited for; matrix products, arithmetic and copies ran while one was open for 0% of the time, Pallas kernels for 0%

profile of v4, /device:TPU:1, one launch (start us, length us, event | category | flops | bytes accessed | tf_op | source)
XLA Modules:
  0.0 38.1 jit_solution(8244518524498790583)
XLA Ops:
  0.0 6.5 %shard_map.37 = (f32[8,40,128]{2,1,0:T(8,128)S(1)}, f32[8,40,128]{2,1,0:T(8,128)S(1)}, s32[8,128]{1,0:T(8,128)S(1)}, s32[8,128]{1,0:T(8,128)S(1)}) custom-call(bf16[8,2,32,2048]{3,2,1,0:T(8,128)(2,1)} %x_hbm.1, s32[2,128]{1,0:T(2,128)} %bitcast.9, s32[16,128]{1,0:T(8,128)} %bitcast.8), custom_call_target="tpu_custom_call" | custom-call | tf_op jit(solution)/shard_map/pallas_call | solution.py:342
  6.5 3.3 %collective-permute-start = (f32[8,40,128]{2,1,0:T(8,128)S(1)}, f32[8,40,128]{2,1,0:T(8,128)S(1)}, u32[]{:S(2)}, u32[]{:S(2)}) collective-permute-start(f32[8,40,128]{2,1,0:T(8,128)S(1)} %get-tuple-element.11), channel_id=1, source_target_pairs={{0,1},{1,0},{2,3},{3,2},{4,5},{5,4},{6,7},{7,6},{8,9},{9,8},{10,11... | collective-permute-start | bytes 491528 | tf_op jit(solution)/shard_map/ppermute | solution.py:363
  9.8 1.0 %collective-permute-done.theirs_ref = f32[8,40,128]{2,1,0:T(8,128)S(1)} collective-permute-done((f32[8,40,128]{2,1,0:T(8,128)S(1)}, f32[8,40,128]{2,1,0:T(8,128)S(1)}, u32[]{:S(2)}, u32[]{:S(2)}) %collective-permute-start) | collective-permute-done | bytes 163872 | tf_op jit(solution)/shard_map/ppermute | solution.py:363
  10.8 0.2 shard_map.38
  11.0 0.2 copy.4
  11.2 25.5 %all_to_all.5 = f32[128,1,384]{2,1,0:T(1,128)S(1)} all-to-all(f32[128,1,384]{2,1,0:T(1,128)S(1)} %copy.4), channel_id=1, replica_groups=mesh['z'=8,'y'=4,'x'=4,'c'=2] {'x','z','y'}, dimensions={0} | all-to-all | bytes 393216 | tf_op jit(solution)/shard_map/all_to_all | solution.py:372
  36.7 1.4 %shard_map.39 = f32[8,1024]{1,0:T(8,128)} custom-call(s32[8,128]{1,0:T(8,128)S(1)} %get-tuple-element.9.walk_ref, f32[128,384]{1,0:T(8,128)S(1)} %bitcast.7), custom_call_target="tpu_custom_call" | custom-call | tf_op jit(solution)/shard_map/pallas_call | solution.py:375
  (1 shorter events, 0.0 us)
Async XLA Ops:
  6.5 4.3 %collective-permute-start = (f32[8,40,128]{2,1,0:T(8,128)S(1)}, f32[8,40,128]{2,1,0:T(8,128)S(1)}, u32[]{:S(2)}, u32[]{:S(2)}) collective-permute-start(f32[8,40,128]{2,1,0:T(8,128)S(1)} %get-tuple-element.11), channel_id=1, source_target_pairs={{0,1},{1,0},{2,3},{3,2},{4,5},{5,4},{6,7},{7,6},{8,9},{9,8},{10,11... | collective-permute-start | bytes 491528 | tf_op jit(solution)/shard_map/ppermute | solution.py:363

commit v5 on v4

--- a/solution.py
+++ b/solution.py
@@ -75,10 +75,14 @@
     odd_ref, even_ref, wodd_ref, weven_ref,
 ):
     slow, core = places()
-    for at in range(0, 512, 32):
-        fine = cos_sin(((iota((32, 128), 0) + at) * (iota((32, 128), 1) & 7)) & (F - 1), F)
-        fine_ref[0, at : at + 32, :] = fine[0]
-        fine_ref[1, at : at + 32, :] = fine[1]
+    zero = slow >> 8
+    fine = cos_sin((iota((8, 512), 1) * iota((8, 512), 0)) & (F - 1), F)
+    blank = jnp.zeros((120, 128), f32)
+    for part in range(2):
+        for at in range(0, 512, 128):
+            fine_ref[part, at : at + 128, :] = jnp.concatenate(
+                [fine[part][:, at : at + 128], blank], axis=0
+            ).T
 
     copies[0].wait()
     order = order_ref[...].astype(f32).astype(bf16)
@@ -93,18 +97,23 @@
         [jnp.where(flip, halves[1], halves[0]), jnp.where(flip, halves[0], halves[1])], axis=1
     ).astype(jnp.int32)
 
-    for at in range(0, BANDS, 16):
-        turns = ((iota((16, BANDS), 0) + at) * bands) & (BANDS - 1)
-        band = cos_sin(turns, BANDS)
-        band_ref[0, at : at + 16, :] = band[0]
-        band_ref[1, at : at + 16, :] = band[1]
+    steps = [(bands * k) & 3 for k in range(4)]
+    real = [jnp.where(k == 0, 1.0, jnp.where(k == 2, -1.0, 0.0)) for k in steps]
+    imag = [jnp.where(k == 1, 1.0, jnp.where(k == 3, -1.0, 0.0)) for k in steps]
+    for at in range(0, 64, 16):
+        c, s = cos_sin(((iota((16, BANDS), 0) + at) * bands) & (BANDS - 1), BANDS)
+        band_ref[0, at : at + 16, :] = c
+        band_ref[1, at : at + 16, :] = s
+        for k in range(1, 4):
+            band_ref[0, k * 64 + at : k * 64 + at + 16, :] = c * real[k] - s * imag[k]
+            band_ref[1, k * 64 + at : k * 64 + at + 16, :] = s * real[k] + c * imag[k]
 
     def table(j, half, row):
         at = half * 256 + row
-        fc = fine_ref[0, at : at + 16, j : j + 1]
-        fs = fine_ref[1, at : at + 16, j : j + 1]
-        bc = band_ref[0, row : row + 16, :]
-        bs = band_ref[1, row : row + 16, :]
+        fc = fine_ref[0 + zero, at : at + 16, j : j + 1]
+        fs = fine_ref[1 + zero, at : at + 16, j : j + 1]
+        bc = band_ref[0 + zero, row : row + 16, :]
+        bs = band_ref[1 + zero, row : row + 16, :]
         c = (bc * fc - bs * fs).astype(bf16)
         s = (bs * fc + bc * fs).astype(bf16)
         if j % 2:
@@ -161,15 +170,18 @@
     def walks_of():
         copies[1].wait()
         rows16 = iota((16, BANDS), 0) == (bands >> 4)
+        pick = iota((128, BANDS), 0) == ((bands & 15) << 3)
+        held = walk_ref[...].astype(f32)
+        shifts = jnp.concatenate(
+            [held if j == 0 else pltpu.roll(held, 128 - j, 1) for j in range(8)], axis=0
+        )
+        got = jnp.dot(
+            shifts.astype(bf16), pick.astype(f32).astype(bf16), preferred_element_type=f32
+        )
         walks = []
         for j in range(8):
-            pick = iota((128, BANDS), 0) == (((bands & 15) << 3) + j)
-            got = jnp.dot(
-                walk_ref[...].astype(f32).astype(bf16),
-                pick.astype(f32).astype(bf16),
-                preferred_element_type=f32,
-            )
-            walk = jnp.sum(jnp.where(rows16, got, 0.0), axis=0, keepdims=True).astype(jnp.int32)
+            mine = jnp.where(rows16, got[j * 16 : j * 16 + 16], 0.0)
+            walk = jnp.sum(mine, axis=0, keepdims=True).astype(jnp.int32)
             own_ref[j : j + 1, :] = walk[:, 128:]
             walks.append(walk)
         return walks
@@ -184,8 +196,8 @@
         for i in range(PER):
             own = jnp.where(
                 ahead,
-                power_ref[j, i * ROWS : (i + 1) * ROWS, lanes],
-                power_ref[j, (7 - i) * ROWS : (8 - i) * ROWS, lanes],
+                power_ref[j + zero, i * ROWS : (i + 1) * ROWS, lanes],
+                power_ref[j + zero, (7 - i) * ROWS : (8 - i) * ROWS, lanes],
             )
             own = jnp.concatenate([own, rim], axis=0)
             if i == 0:
@@ -212,9 +224,9 @@
             for k in range(0, depth, 256):
                 for place, j in enumerate(pair):
                     if j % 2:
-                        left, index, w = odd_ref, (j // 2) % 2, wodd_ref[j // 2, k : k + 256]
+                        left, index, w = odd_ref, (j // 2) % 2 + zero, wodd_ref[j // 2 + zero, k : k + 256]
                     else:
-                        left, index, w = even_ref, j // 2, weven_ref[j // 2, k : k + 256]
+                        left, index, w = even_ref, j // 2 + zero, weven_ref[j // 2 + zero, k : k + 256]
                     rows = jnp.concatenate(
                         [
                             left[index, level, at : at + count, k : k + 256],
@@ -259,12 +271,15 @@
     for g in range(4, 8):
         copies[2 + g].wait()
     products((1, 5), 128, 0, folds(fold_odd, range(4, 8), 4) + tables(3, 7))
-    products((1, 5), 128, 128, folds(fold_even, range(4), 2) + tables(0, 4))
-    products((3, 7), 256, 0, folds(fold_even, range(4, 8), 2) + tables(2, 6) + aligns(1, 5))
-    products((0, 4), 256, 0, aligns(3, 7))
-    products((2, 6), 256, 0, aligns(0, 4))
-    for task in aligns(2, 6):
-        task()
+    products((1, 5), 128, 128, folds(fold_even, range(4), 2))
+    products((3, 7), 256, 0, folds(fold_even, range(4, 8), 2) + tables(0, 4, 2, 6) + aligns(1, 5))
+
+    @pl.when(zero == 0)
+    def evens():
+        products((0, 4), 256, 0, aligns(3, 7))
+        products((2, 6), 256, 0, aligns(0, 4))
+        for task in aligns(2, 6):
+            task()
 
 
 def pair_kernel(mine_ref, theirs_ref, meet_ref, out_ref, flat_ref):

time: 38.2 us -> 38.8 us (1.016)
  Pallas kernels: 8.04 us -> 8.6 us
    pallas_call x1, Pallas kernels: 6.46 us -> 7.02 us  [on_device(): pl.pallas_call(spectra_kernel, out_shape=(block, block, row, row), in_spe...]
where the time goes in v5:
time: 38.8 us; the launch traced here: 38.6 us
  blocking collectives  25.5 us (66%)
  Pallas kernels  8.6 us (22%)
  starting transfers between devices  3.29 us (8%)
  waiting for transfers between devices  1.03 us (3%)
    all_to_all x1, blocking collectives, on_device(): lax.all_to_all(messages.reshape(128, 1, 384), ('x', 'z', 'y'), split_axis...  25.5 us
    pallas_call x1, Pallas kernels, on_device(): pl.pallas_call(spectra_kernel, out_shape=(block, block, row, row), in_spe...  7.02 us
    ppermute x1, starting transfers between devices, on_device(): theirs = lax.ppermute(send, 'c', [(0, 1), (1, 0)])  3.29 us
    pallas_call x1, Pallas kernels, on_device(): pl.pallas_call(join_kernel, out_shape=jax.ShapeDtypeStruct((8, 1024), f32...  1.39 us
    ppermute x1, waiting for transfers between devices, on_device(): theirs = lax.ppermute(send, 'c', [(0, 1), (1, 0)])  1.03 us
  transfers between devices with their start and end apart: 1, of which 1 were waited for; matrix products, arithmetic and copies ran while one was open for 0% of the time, Pallas kernels for 0%

profile of v5, /device:TPU:1, one launch (start us, length us, event | category | flops | bytes accessed | tf_op | source)
XLA Modules:
  0.0 38.6 jit_solution(14532033581035949269)
XLA Ops:
  0.0 7.0 %shard_map.37 = (f32[8,40,128]{2,1,0:T(8,128)S(1)}, f32[8,40,128]{2,1,0:T(8,128)S(1)}, s32[8,128]{1,0:T(8,128)S(1)}, s32[8,128]{1,0:T(8,128)S(1)}) custom-call(bf16[8,2,32,2048]{3,2,1,0:T(8,128)(2,1)} %x_hbm.1, s32[2,128]{1,0:T(2,128)} %bitcast.9, s32[16,128]{1,0:T(8,128)} %bitcast.8), custom_call_target="tpu_custom_call" | custom-call | tf_op jit(solution)/shard_map/pallas_call | solution.py:357
  7.0 3.3 %collective-permute-start = (f32[8,40,128]{2,1,0:T(8,128)S(1)}, f32[8,40,128]{2,1,0:T(8,128)S(1)}, u32[]{:S(2)}, u32[]{:S(2)}) collective-permute-start(f32[8,40,128]{2,1,0:T(8,128)S(1)} %get-tuple-element.11), channel_id=1, source_target_pairs={{0,1},{1,0},{2,3},{3,2},{4,5},{5,4},{6,7},{7,6},{8,9},{9,8},{10,11... | collective-permute-start | bytes 491528 | tf_op jit(solution)/shard_map/ppermute | solution.py:378
  10.3 1.0 %collective-permute-done.theirs_ref = f32[8,40,128]{2,1,0:T(8,128)S(1)} collective-permute-done((f32[8,40,128]{2,1,0:T(8,128)S(1)}, f32[8,40,128]{2,1,0:T(8,128)S(1)}, u32[]{:S(2)}, u32[]{:S(2)}) %collective-permute-start) | collective-permute-done | bytes 163872 | tf_op jit(solution)/shard_map/ppermute | solution.py:378
  11.3 0.2 shard_map.38
  11.5 0.2 copy.4
  11.7 25.5 %all_to_all.5 = f32[128,1,384]{2,1,0:T(1,128)S(1)} all-to-all(f32[128,1,384]{2,1,0:T(1,128)S(1)} %copy.4), channel_id=1, replica_groups=mesh['z'=8,'y'=4,'x'=4,'c'=2] {'x','z','y'}, dimensions={0} | all-to-all | bytes 393216 | tf_op jit(solution)/shard_map/all_to_all | solution.py:387
  37.3 1.4 %shard_map.39 = f32[8,1024]{1,0:T(8,128)} custom-call(s32[8,128]{1,0:T(8,128)S(1)} %get-tuple-element.9.walk_ref, f32[128,384]{1,0:T(8,128)S(1)} %bitcast.7), custom_call_target="tpu_custom_call" | custom-call | tf_op jit(solution)/shard_map/pallas_call | solution.py:390
  (1 shorter events, 0.0 us)
Async XLA Ops:
  7.0 4.3 %collective-permute-start = (f32[8,40,128]{2,1,0:T(8,128)S(1)}, f32[8,40,128]{2,1,0:T(8,128)S(1)}, u32[]{:S(2)}, u32[]{:S(2)}) collective-permute-start(f32[8,40,128]{2,1,0:T(8,128)S(1)} %get-tuple-element.11), channel_id=1, source_target_pairs={{0,1},{1,0},{2,3},{3,2},{4,5},{5,4},{6,7},{7,6},{8,9},{9,8},{10,11... | collective-permute-start | bytes 491528 | tf_op jit(solution)/shard_map/ppermute | solution.py:378

commit v6 on v5

--- a/solution.py
+++ b/solution.py
@@ -110,10 +110,10 @@
 
     def table(j, half, row):
         at = half * 256 + row
-        fc = fine_ref[0 + zero, at : at + 16, j : j + 1]
-        fs = fine_ref[1 + zero, at : at + 16, j : j + 1]
-        bc = band_ref[0 + zero, row : row + 16, :]
-        bs = band_ref[1 + zero, row : row + 16, :]
+        fc = fine_ref[0, at : at + 16, j : j + 1]
+        fs = fine_ref[1, at : at + 16, j : j + 1]
+        bc = band_ref[0, row : row + 16, :]
+        bs = band_ref[1, row : row + 16, :]
         c = (bc * fc - bs * fs).astype(bf16)
         s = (bs * fc + bc * fs).astype(bf16)
         if j % 2:
@@ -196,8 +196,8 @@
         for i in range(PER):
             own = jnp.where(
                 ahead,
-                power_ref[j + zero, i * ROWS : (i + 1) * ROWS, lanes],
-                power_ref[j + zero, (7 - i) * ROWS : (8 - i) * ROWS, lanes],
+                power_ref[j, i * ROWS : (i + 1) * ROWS, lanes],
+                power_ref[j, (7 - i) * ROWS : (8 - i) * ROWS, lanes],
             )
             own = jnp.concatenate([own, rim], axis=0)
             if i == 0:
@@ -224,9 +224,9 @@
             for k in range(0, depth, 256):
                 for place, j in enumerate(pair):
                     if j % 2:
-                        left, index, w = odd_ref, (j // 2) % 2 + zero, wodd_ref[j // 2 + zero, k : k + 256]
+                        left, index, w = odd_ref, (j // 2) % 2, wodd_ref[j // 2, k : k + 256]
                     else:
-                        left, index, w = even_ref, j // 2 + zero, weven_ref[j // 2 + zero, k : k + 256]
+                        left, index, w = even_ref, j // 2, weven_ref[j // 2, k : k + 256]
                     rows = jnp.concatenate(
                         [
                             left[index, level, at : at + count, k : k + 256],
@@ -271,15 +271,12 @@
     for g in range(4, 8):
         copies[2 + g].wait()
     products((1, 5), 128, 0, folds(fold_odd, range(4, 8), 4) + tables(3, 7))
-    products((1, 5), 128, 128, folds(fold_even, range(4), 2))
-    products((3, 7), 256, 0, folds(fold_even, range(4, 8), 2) + tables(0, 4, 2, 6) + aligns(1, 5))
-
-    @pl.when(zero == 0)
-    def evens():
-        products((0, 4), 256, 0, aligns(3, 7))
-        products((2, 6), 256, 0, aligns(0, 4))
-        for task in aligns(2, 6):
-            task()
+    products((1, 5), 128, 128, folds(fold_even, range(8), 2))
+    products((3, 7), 256, 0, tables(0, 4, 2, 6) + aligns(1, 5))
+    products((0, 4), 256, 0, aligns(3, 7))
+    products((2, 6), 256, 0, aligns(0, 4))
+    for task in aligns(2, 6):
+        task()
 
 
 def pair_kernel(mine_ref, theirs_ref, meet_ref, out_ref, flat_ref):

time: 38.8 us -> 38.1 us (0.982)
  Pallas kernels: 8.6 us -> 7.94 us
    pallas_call x1, Pallas kernels: 7.02 us -> 6.37 us  [on_device(): pl.pallas_call(spectra_kernel, out_shape=(block, block, row, row), in_spe...]
where the time goes in v6:
time: 38.1 us; the launch traced here: 38 us
  blocking collectives  25.5 us (67%)
  Pallas kernels  7.94 us (21%)
  starting transfers between devices  3.29 us (9%)
  waiting for transfers between devices  1.03 us (3%)
    all_to_all x1, blocking collectives, on_device(): lax.all_to_all(messages.reshape(128, 1, 384), ('x', 'z', 'y'), split_axis...  25.5 us
    pallas_call x1, Pallas kernels, on_device(): pl.pallas_call(spectra_kernel, out_shape=(block, block, row, row), in_spe...  6.37 us
    ppermute x1, starting transfers between devices, on_device(): theirs = lax.ppermute(send, 'c', [(0, 1), (1, 0)])  3.29 us
    pallas_call x1, Pallas kernels, on_device(): pl.pallas_call(join_kernel, out_shape=jax.ShapeDtypeStruct((8, 1024), f32...  1.39 us
    ppermute x1, waiting for transfers between devices, on_device(): theirs = lax.ppermute(send, 'c', [(0, 1), (1, 0)])  1.03 us
  transfers between devices with their start and end apart: 1, of which 1 were waited for; matrix products, arithmetic and copies ran while one was open for 0% of the time, Pallas kernels for 0%

profile of v6, /device:TPU:1, one launch (start us, length us, event | category | flops | bytes accessed | tf_op | source)
XLA Modules:
  0.0 38.0 jit_solution(12010969294867534635)
XLA Ops:
  0.0 6.4 %shard_map.37 = (f32[8,40,128]{2,1,0:T(8,128)S(1)}, f32[8,40,128]{2,1,0:T(8,128)S(1)}, s32[8,128]{1,0:T(8,128)S(1)}, s32[8,128]{1,0:T(8,128)S(1)}) custom-call(bf16[8,2,32,2048]{3,2,1,0:T(8,128)(2,1)} %x_hbm.1, s32[2,128]{1,0:T(2,128)} %bitcast.9, s32[16,128]{1,0:T(8,128)} %bitcast.8), custom_call_target="tpu_custom_call" | custom-call | tf_op jit(solution)/shard_map/pallas_call | solution.py:354
  6.4 3.3 %collective-permute-start = (f32[8,40,128]{2,1,0:T(8,128)S(1)}, f32[8,40,128]{2,1,0:T(8,128)S(1)}, u32[]{:S(2)}, u32[]{:S(2)}) collective-permute-start(f32[8,40,128]{2,1,0:T(8,128)S(1)} %get-tuple-element.11), channel_id=1, source_target_pairs={{0,1},{1,0},{2,3},{3,2},{4,5},{5,4},{6,7},{7,6},{8,9},{9,8},{10,11... | collective-permute-start | bytes 491528 | tf_op jit(solution)/shard_map/ppermute | solution.py:375
  9.7 1.0 %collective-permute-done.theirs_ref = f32[8,40,128]{2,1,0:T(8,128)S(1)} collective-permute-done((f32[8,40,128]{2,1,0:T(8,128)S(1)}, f32[8,40,128]{2,1,0:T(8,128)S(1)}, u32[]{:S(2)}, u32[]{:S(2)}) %collective-permute-start) | collective-permute-done | bytes 163872 | tf_op jit(solution)/shard_map/ppermute | solution.py:375
  10.7 0.2 shard_map.38
  10.9 0.2 copy.4
  11.1 25.5 %all_to_all.5 = f32[128,1,384]{2,1,0:T(1,128)S(1)} all-to-all(f32[128,1,384]{2,1,0:T(1,128)S(1)} %copy.4), channel_id=1, replica_groups=mesh['z'=8,'y'=4,'x'=4,'c'=2] {'x','z','y'}, dimensions={0} | all-to-all | bytes 393216 | tf_op jit(solution)/shard_map/all_to_all | solution.py:384
  36.6 1.4 %shard_map.39 = f32[8,1024]{1,0:T(8,128)} custom-call(s32[8,128]{1,0:T(8,128)S(1)} %get-tuple-element.9.walk_ref, f32[128,384]{1,0:T(8,128)S(1)} %bitcast.7), custom_call_target="tpu_custom_call" | custom-call | tf_op jit(solution)/shard_map/pallas_call | solution.py:387
  (1 shorter events, 0.0 us)
Async XLA Ops:
  6.4 4.3 %collective-permute-start = (f32[8,40,128]{2,1,0:T(8,128)S(1)}, f32[8,40,128]{2,1,0:T(8,128)S(1)}, u32[]{:S(2)}, u32[]{:S(2)}) collective-permute-start(f32[8,40,128]{2,1,0:T(8,128)S(1)} %get-tuple-element.11), channel_id=1, source_target_pairs={{0,1},{1,0},{2,3},{3,2},{4,5},{5,4},{6,7},{7,6},{8,9},{9,8},{10,11... | collective-permute-start | bytes 491528 | tf_op jit(solution)/shard_map/ppermute | solution.py:375

commit v7 on v6

--- a/solution.py
+++ b/solution.py
@@ -12,6 +12,7 @@
 ROWS = 32
 PER = 8
 WIN = 40
+HALF_ROOT = math.sqrt(0.5)
 GRANT = 40 << 20
 SCALE = 1.0 / (64 * F)
 f32 = jnp.float32
@@ -62,8 +63,9 @@
             copies, send_ref, keep_ref, meet_ref, own_ref,
             x_ref, order_ref, walk_ref, band_ref, fine_ref, power_ref, *refs
         ),
-        packed(2, 2, 512, 1024),
-        packed(4, 2, 512, 512),
+        packed(2, 512, 1024),
+        packed(4, 512, 512),
+        packed(8, 512, 512),
         packed(4, 1024, 256),
         packed(4, 512, 256),
     )
@@ -72,7 +74,7 @@
 def spectra(
     copies, send_ref, keep_ref, meet_ref, own_ref,
     x_ref, order_ref, walk_ref, band_ref, fine_ref, power_ref,
-    odd_ref, even_ref, wodd_ref, weven_ref,
+    odd_ref, even_ref, low_ref, wodd_ref, weven_ref,
 ):
     slow, core = places()
     zero = slow >> 8
@@ -123,16 +125,19 @@
             weven_ref[j // 2, at : at + 16, :] = c
             weven_ref[j // 2, 256 + at : 256 + at + 16, :] = s
 
-    def put(ref, index, row, col, depth, zr, zi):
-        rh = zr.astype(bf16)
-        ih = zi.astype(bf16)
-        rl = (zr - rh.astype(f32)).astype(bf16)
-        il = (zi - ih.astype(f32)).astype(bf16)
-        for level, (re, im) in enumerate(((rh, ih), (rl, il))):
-            ref[index, level, row : row + 16, col : col + 128] = re
-            ref[index, level, row : row + 16, depth + col : depth + col + 128] = im
-            ref[index, level, 256 + row : 256 + row + 16, col : col + 128] = im
-            ref[index, level, 256 + row : 256 + row + 16, depth + col : depth + col + 128] = -re
+    def put(ref, index, row, col, depth, re, im):
+        ref[index, row : row + 16, col : col + 128] = re
+        ref[index, row : row + 16, depth + col : depth + col + 128] = im
+        ref[index, 256 + row : 256 + row + 16, col : col + 128] = im
+        ref[index, 256 + row : 256 + row + 16, depth + col : depth + col + 128] = -re
+
+    def high(ref, index, row, col, depth, zr, zi):
+        rh, ih = zr.astype(bf16), zi.astype(bf16)
+        put(ref, index, row, col, depth, rh, ih)
+        return zr - rh.astype(f32), zi - ih.astype(f32)
+
+    def low(j, row, col, zr, zi):
+        put(low_ref, j, row, col, 256, zr.astype(bf16), zi.astype(bf16))
 
     def quarters(g, part, cb):
         return [
@@ -145,13 +150,26 @@
             for c in range(2)
         ]
 
-    def fold_odd(g, part, cb):
-        re, im = quarters(g, part, cb)
-        dr, di = re[0] - re[2], im[0] - im[2]
-        er, ei = re[1] - re[3], im[1] - im[3]
+    def fold_odd(g, part, pair):
         row = g * ROWS + part * 16
-        put(odd_ref, 0, row, cb * 128, 512, dr + ei, di - er)
-        put(odd_ref, 1, row, cb * 128, 512, dr - ei, di + er)
+        rests = []
+        for cb in (pair, pair + 2):
+            re, im = quarters(g, part, cb)
+            dr, di = re[0] - re[2], im[0] - im[2]
+            er, ei = re[1] - re[3], im[1] - im[3]
+            rests.append(
+                (
+                    high(odd_ref, 0, row, cb * 128, 512, dr + ei, di - er),
+                    high(odd_ref, 1, row, cb * 128, 512, dr - ei, di + er),
+                )
+            )
+        for q in range(2):
+            (ar, ai), (br, bi) = rests[0][q], rests[1][q]
+            cr, ci = (br + bi) * HALF_ROOT, (bi - br) * HALF_ROOT
+            if q == 1:
+                cr, ci = ci, -cr
+            low(1 + 2 * q, row, pair * 128, ar + cr, ai + ci)
+            low(5 + 2 * q, row, pair * 128, ar - cr, ai - ci)
 
     def fold_even(g, part, pair):
         row = g * ROWS + part * 16
@@ -162,10 +180,10 @@
             ur, ui = re[1] + re[3], im[1] + im[3]
             zs.append((sr + ur, si + ui, sr - ur, si - ui))
         (ar, ai, cr, ci), (br, bi, dr, di) = zs
-        put(even_ref, 0, row, pair * 128, 256, ar + br, ai + bi)
-        put(even_ref, 2, row, pair * 128, 256, ar - br, ai - bi)
-        put(even_ref, 1, row, pair * 128, 256, cr + di, ci - dr)
-        put(even_ref, 3, row, pair * 128, 256, cr - di, ci + dr)
+        low(0, row, pair * 128, *high(even_ref, 0, row, pair * 128, 256, ar + br, ai + bi))
+        low(4, row, pair * 128, *high(even_ref, 2, row, pair * 128, 256, ar - br, ai - bi))
+        low(2, row, pair * 128, *high(even_ref, 1, row, pair * 128, 256, cr + di, ci - dr))
+        low(6, row, pair * 128, *high(even_ref, 3, row, pair * 128, 256, cr - di, ci + dr))
 
     def walks_of():
         copies[1].wait()
@@ -220,26 +238,31 @@
     def products(pair, count, at, side):
         depth = 1024 if pair[0] % 2 else 512
         sums = [None, None]
-        for level in range(2):
-            for k in range(0, depth, 256):
-                for place, j in enumerate(pair):
-                    if j % 2:
-                        left, index, w = odd_ref, (j // 2) % 2, wodd_ref[j // 2, k : k + 256]
-                    else:
-                        left, index, w = even_ref, j // 2, weven_ref[j // 2, k : k + 256]
-                    rows = jnp.concatenate(
-                        [
-                            left[index, level, at : at + count, k : k + 256],
-                            left[index, level, 256 + at : 256 + at + count, k : k + 256],
-                        ],
-                        axis=0,
-                    )
-                    got = jnp.dot(rows, w, preferred_element_type=f32)
-                    sums[place] = got if sums[place] is None else sums[place] + got
-                share = -(-len(side) // (2 * depth // 256 - level * (depth // 256) - k // 256))
-                for task in side[:share]:
-                    task()
-                side = side[share:]
+        steps = [(0, k) for k in range(0, depth, 256)] + [(1, 0), (1, 256)]
+        for done, (level, k) in enumerate(steps):
+            for place, j in enumerate(pair):
+                w_ref = wodd_ref if j % 2 else weven_ref
+                table_row = k * (depth // 512) if level else k
+                w = w_ref[j // 2, table_row : table_row + 256]
+                if level:
+                    left, index = low_ref, j
+                elif j % 2:
+                    left, index = odd_ref, (j // 2) % 2
+                else:
+                    left, index = even_ref, j // 2
+                rows = jnp.concatenate(
+                    [
+                        left[index, at : at + count, k : k + 256],
+                        left[index, 256 + at : 256 + at + count, k : k + 256],
+                    ],
+                    axis=0,
+                )
+                got = jnp.dot(rows, w, preferred_element_type=f32)
+                sums[place] = got if sums[place] is None else sums[place] + got
+            share = -(-len(side) // (len(steps) - done))
+            for task in side[:share]:
+                task()
+            side = side[share:]
         for place, j in enumerate(pair):
             re, im = sums[place][:count], sums[place][count:]
             power_ref[j, at : at + count, :] = re * re + im * im
@@ -266,11 +289,11 @@
     walks = walks_of()
     for g in range(4):
         copies[2 + g].wait()
-    for task in folds(fold_odd, range(4), 4):
+    for task in folds(fold_odd, range(4), 2):
         task()
     for g in range(4, 8):
         copies[2 + g].wait()
-    products((1, 5), 128, 0, folds(fold_odd, range(4, 8), 4) + tables(3, 7))
+    products((1, 5), 128, 0, folds(fold_odd, range(4, 8), 2) + tables(3, 7))
     products((1, 5), 128, 128, folds(fold_even, range(8), 2))
     products((3, 7), 256, 0, tables(0, 4, 2, 6) + aligns(1, 5))
     products((0, 4), 256, 0, aligns(3, 7))

time: 38.1 us -> 37.6 us (0.987)
  Pallas kernels: 7.94 us -> 7.43 us
    pallas_call x1, Pallas kernels: 6.37 us -> 5.85 us  [on_device(): pl.pallas_call(spectra_kernel, out_shape=(block, block, row, row), in_spe...]
where the time goes in v7:
time: 37.6 us; the launch traced here: 37.5 us
  blocking collectives  25.5 us (68%)
  Pallas kernels  7.43 us (20%)
  starting transfers between devices  3.29 us (9%)
  waiting for transfers between devices  1.03 us (3%)
    all_to_all x1, blocking collectives, on_device(): lax.all_to_all(messages.reshape(128, 1, 384), ('x', 'z', 'y'), split_axis...  25.5 us
    pallas_call x1, Pallas kernels, on_device(): pl.pallas_call(spectra_kernel, out_shape=(block, block, row, row), in_spe...  5.85 us
    ppermute x1, starting transfers between devices, on_device(): theirs = lax.ppermute(send, 'c', [(0, 1), (1, 0)])  3.29 us
    pallas_call x1, Pallas kernels, on_device(): pl.pallas_call(join_kernel, out_shape=jax.ShapeDtypeStruct((8, 1024), f32...  1.39 us
    ppermute x1, waiting for transfers between devices, on_device(): theirs = lax.ppermute(send, 'c', [(0, 1), (1, 0)])  1.03 us
  transfers between devices with their start and end apart: 1, of which 1 were waited for; matrix products, arithmetic and copies ran while one was open for 0% of the time, Pallas kernels for 0%

profile of v7, /device:TPU:1, one launch (start us, length us, event | category | flops | bytes accessed | tf_op | source)
XLA Modules:
  0.0 37.5 jit_solution(1833850947292617456)
XLA Ops:
  0.0 5.9 %shard_map.37 = (f32[8,40,128]{2,1,0:T(8,128)S(1)}, f32[8,40,128]{2,1,0:T(8,128)S(1)}, s32[8,128]{1,0:T(8,128)S(1)}, s32[8,128]{1,0:T(8,128)S(1)}) custom-call(bf16[8,2,32,2048]{3,2,1,0:T(8,128)(2,1)} %x_hbm.1, s32[2,128]{1,0:T(2,128)} %bitcast.9, s32[16,128]{1,0:T(8,128)} %bitcast.8), custom_call_target="tpu_custom_call" | custom-call | tf_op jit(solution)/shard_map/pallas_call | solution.py:377
  5.9 3.3 %collective-permute-start = (f32[8,40,128]{2,1,0:T(8,128)S(1)}, f32[8,40,128]{2,1,0:T(8,128)S(1)}, u32[]{:S(2)}, u32[]{:S(2)}) collective-permute-start(f32[8,40,128]{2,1,0:T(8,128)S(1)} %get-tuple-element.11), channel_id=1, source_target_pairs={{0,1},{1,0},{2,3},{3,2},{4,5},{5,4},{6,7},{7,6},{8,9},{9,8},{10,11... | collective-permute-start | bytes 491528 | tf_op jit(solution)/shard_map/ppermute | solution.py:398
  9.1 1.0 %collective-permute-done.theirs_ref = f32[8,40,128]{2,1,0:T(8,128)S(1)} collective-permute-done((f32[8,40,128]{2,1,0:T(8,128)S(1)}, f32[8,40,128]{2,1,0:T(8,128)S(1)}, u32[]{:S(2)}, u32[]{:S(2)}) %collective-permute-start) | collective-permute-done | bytes 163872 | tf_op jit(solution)/shard_map/ppermute | solution.py:398
  10.2 0.2 shard_map.38
  10.4 0.2 copy.4
  10.6 25.5 %all_to_all.5 = f32[128,1,384]{2,1,0:T(1,128)S(1)} all-to-all(f32[128,1,384]{2,1,0:T(1,128)S(1)} %copy.4), channel_id=1, replica_groups=mesh['z'=8,'y'=4,'x'=4,'c'=2] {'x','z','y'}, dimensions={0} | all-to-all | bytes 393216 | tf_op jit(solution)/shard_map/all_to_all | solution.py:407
  36.1 1.4 %shard_map.39 = f32[8,1024]{1,0:T(8,128)} custom-call(s32[8,128]{1,0:T(8,128)S(1)} %get-tuple-element.9.walk_ref, f32[128,384]{1,0:T(8,128)S(1)} %bitcast.7), custom_call_target="tpu_custom_call" | custom-call | tf_op jit(solution)/shard_map/pallas_call | solution.py:410
  (1 shorter events, 0.0 us)
Async XLA Ops:
  5.9 4.3 %collective-permute-start = (f32[8,40,128]{2,1,0:T(8,128)S(1)}, f32[8,40,128]{2,1,0:T(8,128)S(1)}, u32[]{:S(2)}, u32[]{:S(2)}) collective-permute-start(f32[8,40,128]{2,1,0:T(8,128)S(1)} %get-tuple-element.11), channel_id=1, source_target_pairs={{0,1},{1,0},{2,3},{3,2},{4,5},{5,4},{6,7},{7,6},{8,9},{9,8},{10,11... | collective-permute-start | bytes 491528 | tf_op jit(solution)/shard_map/ppermute | solution.py:398
